TPU v7x, 128 devices: a whole 4x4x4 slice. The times are simulated.
128 devices in a mesh: row: 8 (over z, x_lo), col: 16 (over y, x_hi, core).
Axes of the slice: x: 4 (x_hi: 2, x_lo: 2; x = x_hi * 2 + x_lo), y: 4, z: 4, core: 2. Of those that a mesh axis runs over, the one named last changes fastest.
Arguments:
- normal_matrix: float32 [14336, 14336], P(('row', 'col')), may hold values from -90 to 90, as said below
- new_index: int32 [14336], replicated, may hold values from 0 to 14335, each once
- check_vectors: float32 [14336, 1024], P('col'), may hold values from -0.046875 to 0.046875
Outputs:
- tile_layout: float32 [14336, 14336], P('row', 'col')
- check_product: float32 [14336, 1024], P(('row', 'col'))
Inputs may be any that keep to these rules, and one draw needn't show every extreme that they name: normal_matrix is symmetric. new_index[a] is the new index of parameter a; every index 0 to 14335 appears once.
All inputs are finite; a program needn't handle non-finite values.
Results may differ from a plain program's by a relative error of at most 0.000082.
Values sent between devices are 32-bit elements; how exact they have to be, the bound alone decides.
No kernel may reach another device: no remote copies, remote signals or barrier semaphores. Data moves between devices by JAX's collectives and lax.ppermute only.
A program may use at most 128 MiB of HBM per device.

v0:
```python
import jax
import jax.numpy as jnp
from jax import lax
from jax.sharding import PartitionSpec as P

TILE = 128


def new_of_packed(places, groups, stride, tile_size):
    holder = places // stride
    within = places % stride
    return (within // tile_size * groups + holder) * tile_size + within % tile_size


def shards(normal_matrix, new_index, check_vectors):
    row_count = lax.axis_size("row")
    col_count = lax.axis_size("col")
    devices = row_count * col_count
    unknowns = new_index.shape[0]
    slab_rows = normal_matrix.shape[0]
    share = unknowns // devices
    places = jnp.arange(unknowns, dtype=jnp.int32)
    old_of_new = jnp.zeros((unknowns,), jnp.int32).at[new_index].set(places)
    row_pick = old_of_new[new_of_packed(places, row_count, unknowns // row_count, TILE)]
    col_pick = old_of_new[new_of_packed(places, col_count, unknowns // col_count, TILE)]
    gathered = jnp.take(normal_matrix.T, row_pick, axis=0)
    grouped = gathered.reshape(devices, share, slab_rows).transpose(0, 2, 1)
    outgoing = grouped.reshape(devices * slab_rows, share)
    arrived = lax.all_to_all(outgoing, ("row", "col"), split_axis=0, concat_axis=0, tiled=True)
    chosen = jnp.take(arrived, col_pick, axis=0)
    moved = lax.all_to_all(chosen, "col", split_axis=0, concat_axis=1, tiled=True)
    tile_layout = moved.T
    check_product = lax.psum_scatter(
        jnp.dot(
            tile_layout,
            check_vectors,
            precision=lax.Precision.HIGHEST,
            preferred_element_type=jnp.float32,
        ),
        "col",
        scatter_dimension=0,
        tiled=True,
    )
    return (tile_layout, check_product)


def solution(mesh):
    return jax.shard_map(
        shards,
        mesh=mesh,
        in_specs=(P(("row", "col"), None), P(), P("col", None)),
        out_specs=(P("row", "col"), P(("row", "col"), None)),
        check_vma=False,
    )
```

profile of v0, /device:TPU:0, one launch (start us, length us, event | category | flops | bytes accessed | tf_op | source)
XLA Modules:
  0.0 604.7 jit_solution(2627453385167262926)
XLA Ops:
  7.2 0.7 compare_select_fusion.1
  7.9 0.8 compare_select_fusion.4
  8.7 52.9 %scatter_custom_fusion = s32[14336]{0:T(1024)S(1)} fusion(s32[14336]{0:T(1024)S(1)} %compare_select_fusion.4, s32[14336]{0:T(1024)S(1)} %iota.11, s32[]{:T(128)} %constant.71.clone.1), kind=kCustom, calls=%fused_computation.43 | custom fusion | bytes 57348 | tf_op jit(solution)/shard_map/scatter | solution.py:23
  61.6 79.3 %gather_fusion = s32[14336]{0:T(1024)S(1)} fusion(s32[14336]{0:T(1024)S(1)} %scatter_custom_fusion, s32[14336]{0:T(1024)S(1)} %broadcast_clamp_fusion), kind=kCustom, calls=%fused_computation.2 | custom fusion | bytes 172032 | tf_op jit(solution)/shard_map/gather | solution.py:24
  141.0 8.3 %copy.11 = f32[112,14336]{0,1:T(8,128)} copy(f32[112,14336]{1,0:T(8,128)} %param.5) | data formatting | bytes 12845056 | tf_op args[0]
  149.3 51.3 %gather_fusion.2 = f32[14336,112]{1,0:T(8,128)} fusion(f32[14336,112]{1,0:T(8,128)} %bitcast.16, s32[14336]{0:T(1024)S(1)} %fusion.6), kind=kCustom, calls=%fused_computation.clone | custom fusion | bytes 12902400 | tf_op jit(solution)/shard_map/jit(_take)/gather | solution.py:26
  200.6 11.3 %broadcast_select_fusion.1 = f32[14336,112]{1,0:T(8,128)} fusion(f32[14336,112]{1,0:T(8,128)} %gather_fusion.2, pred[14336]{0:T(1024)(128)(4,1)S(1)} %compare_and_fusion.1), kind=kLoop, calls=%fused_computation.6 | loop fusion | flops 1605632 | bytes 12859392 | tf_op jit(solution)/shard_map/jit(_take)/select_n | solution.py:26
  211.9 11.6 %all-to-all-start = ((f32[128,112,112]{1,2,0:T(8,128)}), f32[128,112,112]{1,2,0:T(8,128)}, u32[]{:S(2)}, u32[]{:S(2)}) async-start(f32[128,112,112]{1,2,0:T(8,128)} %bitcast.17), calls=%async_computation | async-start | bytes 14680064 | tf_op jit(solution)/shard_map/all_to_all | solution.py:29
  223.5 0.0 reduce-scatter.2.cloned.1.call-start
  223.6 0.7 compare_select_fusion
  224.3 79.3 %gather_fusion.1 = s32[14336]{0:T(1024)S(1)} fusion(s32[14336]{0:T(1024)S(1)} %scatter_custom_fusion, s32[14336]{0:T(1024)S(1)} %broadcast_clamp_fusion.1), kind=kCustom, calls=%fused_computation.3 | custom fusion | bytes 172032 | tf_op jit(solution)/shard_map/gather | solution.py:25
  303.7 8.8 %all-to-all-done = f32[128,112,112]{1,2,0:T(8,128)} async-done(((f32[128,112,112]{1,2,0:T(8,128)}), f32[128,112,112]{1,2,0:T(8,128)}, u32[]{:S(2)}, u32[]{:S(2)}) %all-to-all-start) | async-done | bytes 6422560 | tf_op jit(solution)/shard_map/all_to_all | solution.py:29
  312.5 8.6 %copy.12 = f32[128,112,112]{2,1,0:T(8,128)} copy(f32[128,112,112]{1,2,0:T(8,128)} %all-to-all-done) | data formatting | bytes 12845056 | tf_op jit(solution)/shard_map/all_to_all | solution.py:29
  321.1 51.3 %gather_fusion.3 = f32[14336,112]{1,0:T(8,128)} fusion(f32[14336,112]{1,0:T(8,128)} %bitcast.15, s32[14336]{0:T(1024)S(1)} %fusion.7), kind=kCustom, calls=%fused_computation.1.clone | custom fusion | bytes 12902400 | tf_op jit(solution)/shard_map/jit(_take)/gather | solution.py:30
  372.3 11.3 %broadcast_select_fusion = f32[14336,112]{1,0:T(8,128)} fusion(f32[14336,112]{1,0:T(8,128)} %gather_fusion.3, pred[14336]{0:T(1024)(128)(4,1)S(1)} %compare_and_fusion), kind=kLoop, calls=%fused_computation.5 | loop fusion | flops 1605632 | bytes 12859392 | tf_op jit(solution)/shard_map/jit(_take)/select_n | solution.py:30
  383.7 8.3 %copy.13 = f32[16,896,112]{1,2,0:T(8,128)} copy(f32[16,896,112]{2,1,0:T(8,128)} %bitcast.18) | data formatting | bytes 12845056 | tf_op jit(solution)/shard_map/all_to_all | solution.py:31
  391.9 0.0 copy-start.1
  391.9 82.3 %all_to_all.28 = f32[16,896,112]{1,2,0:T(8,128)S(1)} all-to-all(f32[16,896,112]{1,2,0:T(8,128)} %copy.13), channel_id=1, replica_groups=mesh['row'=8,'col'=16] {'col'}, dimensions={0} | all-to-all | bytes 12845056 | tf_op jit(solution)/shard_map/all_to_all | solution.py:31
  474.2 0.0 copy-start
  474.2 2.7 copy-done
  477.0 0.0 copy-done.1
  477.0 25.2 %fusion.10 = f32[1792,1024]{1,0:T(8,128)} fusion(f32[896,1792]{0,1:T(8,128)S(1)} %bitcast.19, f32[896,1024]{1,0:T(8,128)S(1)} %copy-done.1), kind=kOutput, calls=%fused_computation.45 | convolution fusion | flops 19730006016 | bytes 17432576 | tf_op jit(solution)/shard_map/dot_general | solution.py:34
  502.2 0.0 reduce-scatter.2.cloned.1.call-update
  502.2 89.6 %reduce-scatter.2.cloned.1.call-done = f32[112,1024]{1,0:T(8,128)} async-done(((f32[1792,1024]{1,0:T(8,128)}), f32[112,1024]{1,0:T(8,128)}) %reduce-scatter.2.cloned.1.call-update) | async-done | bytes 458768 | tf_op jit(solution)/shard_map/reduce_scatter | solution.py:33
  591.8 6.0 copy.15
  (7 shorter events, 0.1 us)
Async XLA Ops:
  211.9 100.6 %all-to-all-start = ((f32[128,112,112]{1,2,0:T(8,128)}), f32[128,112,112]{1,2,0:T(8,128)}, u32[]{:S(2)}, u32[]{:S(2)}) async-start(f32[128,112,112]{1,2,0:T(8,128)} %bitcast.17), calls=%async_computation | async-start | bytes 14680064 | tf_op jit(solution)/shard_map/all_to_all | solution.py:29
  223.5 368.3 %reduce-scatter.2.cloned.1.call-start = ((), (), s32[]{:S(2)}) async-start(), calls=%async_computation.3 | async-start | bytes 7798784 | tf_op jit(solution)/shard_map/reduce_scatter | solution.py:33
  391.9 85.0 %copy-start.1 = (f32[896,1024]{1,0:T(8,128)S(1)}, f32[896,1024]{1,0:T(8,128)}, u32[]{:S(2)}) copy-start(f32[896,1024]{1,0:T(8,128)} %param.7) | copy-start | bytes 11010052
  474.2 2.7 copy-start
Sparse Core Ops, SparseCore 0:
  502.4 89.4 reduce-scatter.1
where the time goes:
time: 606 us; the launch traced here: 605 us
  local copies, waits for them, and re-layouts  348 us (57%)
  waiting for transfers between devices  98.4 us (16%)
  blocking collectives  82.3 us (14%)
  matrix products  25.2 us (4%)
  other arithmetic  25 us (4%)
  between operations  14.1 us (2%)
  starting transfers between devices  11.7 us (2%)
    reduce_scatter x1, waiting for transfers between devices, shards(): lax.psum_scatter(jnp.dot(tile_layout, check_vectors, precision=lax.Precis...  89.6 us
    all_to_all x1, blocking collectives, shards(): lax.all_to_all(chosen, 'col', split_axis=0, concat_axis=1, tiled=True)  82.3 us
    gather x1, local copies, waits for them, and re-layouts, shards(): old_of_new[new_of_packed(places, row_count, unknowns // row_count, TILE)]  79.3 us
    gather x1, local copies, waits for them, and re-layouts, shards(): old_of_new[new_of_packed(places, col_count, unknowns // col_count, TILE)]  79.3 us
    scatter x1, local copies, waits for them, and re-layouts, shards(): old_of_new = jnp.zeros((unknowns,), jnp.int32).at[new_index].set(places)  52.9 us
    gather x1, local copies, waits for them, and re-layouts, shards(): gathered = jnp.take(normal_matrix.T, row_pick, axis=0)  51.3 us
    gather x1, local copies, waits for them, and re-layouts, shards(): chosen = jnp.take(arrived, col_pick, axis=0)  51.3 us
    dot_general x1, matrix products, shards(): jnp.dot(tile_layout, check_vectors, precision=lax.Precision.HIGHEST, pref...  25.2 us
  transfers between devices with their start and end apart: 2, of which 2 were waited for; matrix products, arithmetic and copies ran while one was open for 13% of the time, Pallas kernels for 0%

commit v1 on v0

v1 whole, which is shorter than its diff:
```python
import jax
import jax.numpy as jnp
from jax import lax
from jax.experimental import pallas as pl
from jax.experimental.pallas import tpu as pltpu
from jax.sharding import PartitionSpec as P

TILE = 128
LANES = 128
VMEM = 56 * 1024 * 1024


def scatter_rows(pos_ref, base, src_ref, dst_ref, count, unroll=32):
    def body(i, carry):
        start = i * unroll
        for u in range(unroll):
            dst_ref[pl.ds(pos_ref[base + start + u], 1), :] = src_ref[pl.ds(start + u, 1), :]
        return carry

    lax.fori_loop(0, count // unroll, body, 0)


def group_columns(slab, places, devices):
    share, unknowns = slab.shape
    width = 1024
    steps = unknowns // width
    keep = share - 8
    chunk = LANES - share

    def kernel(pos_ref, x_ref, out_ref, turned, spread):
        step = pl.program_id(0)
        for b in range(width // LANES):
            turned[b * LANES:(b + 1) * LANES, :share] = x_ref[:, b * LANES:(b + 1) * LANES].T
        scatter_rows(pos_ref, step * width, turned, spread, width)

        @pl.when(step == steps - 1)
        def _():
            def pack(d, carry):
                out_ref[d] = spread[pl.ds(pl.multiple_of(d * keep, 8), keep), :]
                extra = spread[pl.ds(pl.multiple_of(devices * keep + d * 8, 8), 8), :]
                for k in range(share // chunk):
                    out_ref[d, 8 * k:8 * k + 8, share:] = extra[:, chunk * k:chunk * (k + 1)]
                return carry

            lax.fori_loop(0, devices, pack, 0)

    return pl.pallas_call(
        kernel,
        grid_spec=pltpu.PrefetchScalarGridSpec(
            num_scalar_prefetch=1,
            grid=(steps,),
            in_specs=[pl.BlockSpec((share, width), lambda g, pos: (0, g))],
            out_specs=pl.BlockSpec((devices, keep, LANES), lambda g, pos: (0, 0, 0)),
            scratch_shapes=[
                pltpu.VMEM((width, LANES), jnp.float32),
                pltpu.VMEM((unknowns, LANES), jnp.float32),
            ],
        ),
        out_shape=jax.ShapeDtypeStruct((devices, keep, LANES), jnp.float32),
        compiler_params=pltpu.CompilerParams(vmem_limit_bytes=VMEM),
        name="group_columns",
    )(places, slab)


def group_rows(blocks, places, groups, share):
    devices, keep, _ = blocks.shape
    unknowns = devices * share
    chunk = LANES - share
    per = 8
    steps = devices // per
    rows = unknowns // groups

    def kernel(pos_ref, x_ref, out_ref, turned, spread):
        step = pl.program_id(0)
        for b in range(per):
            flipped = x_ref[b].T
            turned[b * share:(b + 1) * share, :keep] = flipped[:share]
            for k in range(share // chunk):
                turned[b * share + k * chunk:b * share + (k + 1) * chunk, keep:share] = flipped[share:, 8 * k:8 * k + 8]
        scatter_rows(pos_ref, step * per * share, turned, spread, per * share)

        @pl.when(step == steps - 1)
        def _():
            def turn(g, carry):
                for k in range(rows // LANES):
                    piece = spread[pl.ds(pl.multiple_of(g * rows + k * LANES, LANES), LANES), :]
                    out_ref[g, :, k * LANES:(k + 1) * LANES] = piece.T[:share]
                return carry

            lax.fori_loop(0, groups, turn, 0)

    return pl.pallas_call(
        kernel,
        grid_spec=pltpu.PrefetchScalarGridSpec(
            num_scalar_prefetch=1,
            grid=(steps,),
            in_specs=[pl.BlockSpec((per, keep, LANES), lambda g, pos: (g, 0, 0))],
            out_specs=pl.BlockSpec((groups, share, rows), lambda g, pos: (0, 0, 0)),
            scratch_shapes=[
                pltpu.VMEM((per * share, LANES), jnp.float32),
                pltpu.VMEM((unknowns, LANES), jnp.float32),
            ],
        ),
        out_shape=jax.ShapeDtypeStruct((groups, share, rows), jnp.float32),
        compiler_params=pltpu.CompilerParams(vmem_limit_bytes=VMEM),
        name="group_rows",
    )(places, blocks)


def tile_and_product(turned, vectors, core, share):
    columns, rows = turned.shape
    width = vectors.shape[1]
    high = 256 if rows % 256 == 0 else 128
    pairs = rows // (2 * share)

    def split(x):
        hi = x.astype(jnp.bfloat16)
        return hi, (x - hi.astype(jnp.float32)).astype(jnp.bfloat16)

    def kernel(core_ref, x_ref, v_ref, tile_ref, other_ref, mine_ref, v_hi, v_lo):
        step = pl.program_id(0)

        @pl.when(step == 0)
        def _():
            v_hi[...], v_lo[...] = split(v_ref[...])
            for k in range(rows // LANES):
                tile_ref[k * LANES:(k + 1) * LANES, :] = x_ref[:, k * LANES:(k + 1) * LANES].T

        x = tile_ref[pl.ds(pl.multiple_of(step * 2 * share, 8), 2 * share), :]
        hi, lo = split(x)
        part = (
            jnp.dot(hi, v_hi[...], preferred_element_type=jnp.float32)
            + jnp.dot(hi, v_lo[...], preferred_element_type=jnp.float32)
            + jnp.dot(lo, v_hi[...], preferred_element_type=jnp.float32)
        )
        first, second = part[:share], part[share:]
        even = core_ref[0] == 0
        other_ref[0] = jnp.where(even, second, first)
        mine_ref[0] = jnp.where(even, first, second)

    half = jax.ShapeDtypeStruct((pairs, share, width), jnp.float32)
    half_spec = pl.BlockSpec((1, share, width), lambda g, core: (g, 0, 0))
    return pl.pallas_call(
        kernel,
        grid_spec=pltpu.PrefetchScalarGridSpec(
            num_scalar_prefetch=1,
            grid=(pairs,),
            in_specs=[
                pl.BlockSpec((columns, rows), lambda g, core: (0, 0)),
                pl.BlockSpec((columns, width), lambda g, core: (0, 0)),
            ],
            out_specs=[pl.BlockSpec((rows, columns), lambda g, core: (0, 0)), half_spec, half_spec],
            scratch_shapes=[
                pltpu.VMEM((columns, width), jnp.bfloat16),
                pltpu.VMEM((columns, width), jnp.bfloat16),
            ],
        ),
        out_shape=[jax.ShapeDtypeStruct((rows, columns), jnp.float32), half, half],
        compiler_params=pltpu.CompilerParams(vmem_limit_bytes=VMEM),
        name="tile_and_product",
    )(core, turned, vectors)


def shards(normal_matrix, new_index, check_vectors):
    row_count = lax.axis_size("row")
    col_count = lax.axis_size("col")
    devices = row_count * col_count
    share, unknowns = normal_matrix.shape
    keep = share - 8

    tile, lane = new_index // TILE, new_index % TILE
    within_col = tile // col_count * TILE + lane
    block = within_col // share * col_count + tile % col_count
    place = within_col % share
    column_places = jnp.where(
        place < keep, block * keep + place, devices * keep + block * 8 + place - keep
    )
    row_places = tile % row_count * (unknowns // row_count) + tile // row_count * TILE + lane

    outgoing = group_columns(normal_matrix, column_places, devices)
    arrived = lax.all_to_all(outgoing, ("row", "col"), split_axis=0, concat_axis=0, tiled=True)
    chosen = group_rows(arrived, row_places, row_count, share)
    moved = lax.all_to_all(chosen, "row", split_axis=0, concat_axis=0, tiled=True)
    turned = moved.reshape(row_count * share, unknowns // row_count)

    me = lax.axis_index("col")
    core = (me % 2).astype(jnp.int32).reshape(1)
    tile_layout, other, mine = tile_and_product(turned, check_vectors, core, share)
    swap = [(i, i ^ 1) for i in range(col_count)]
    both = mine + lax.ppermute(other, "col", swap)
    groups = [list(range(p, col_count, 2)) for p in range(2)]
    parts = lax.all_to_all(both, "col", split_axis=0, concat_axis=0, axis_index_groups=groups, tiled=True)
    return tile_layout, parts.sum(axis=0)


def solution(mesh):
    return jax.shard_map(
        shards,
        mesh=mesh,
        in_specs=(P(("row", "col"), None), P(), P("col", None)),
        out_specs=(P("row", "col"), P(("row", "col"), None)),
        check_vma=False,
    )
```

time: 606 us -> 314 us (0.52)
  local copies, waits for them, and re-layouts: 348 us -> 0 us
  Pallas kernels: 0 us -> 78.7 us
  blocking collectives: 82.3 us -> 142 us
  matrix products: 25.2 us -> 0 us
  waiting for transfers between devices: 98.4 us -> 80.1 us
  other arithmetic: 25 us -> 7.7 us
  between operations: 14.1 us -> 0.66 us
  starting transfers between devices: 11.7 us -> 4.76 us
    gather x4 -> x0, local copies, waits for them, and re-layouts: 261 us -> none  [the longest x1 79.3 us: shards(): old_of_new[new_of_packed(places, row_count, unknowns // row_count, TILE)]]
    reduce_scatter x1 -> x0, waiting for transfers between devices: 89.6 us -> none  [shards(): lax.psum_scatter(jnp.dot(tile_layout, check_vectors, precision=lax.Precis...]
    pallas_call x0 -> x3, Pallas kernels: none -> 78.7 us  [the longest x1 31.2 us: group_columns(): pl.pallas_call(kernel, grid_spec=pltpu.PrefetchScalarGridSpec(num_scalar_...]
    all_to_all x1, waiting for transfers between devices: 8.8 us -> 73.5 us  [shards(): lax.all_to_all(chosen, 'row', split_axis=0, concat_axis=0, tiled=True)]
    all_to_all x1 -> x2, blocking collectives: 82.3 us -> 142 us  [the longest x1 91.6 us: shards(): lax.all_to_all(outgoing, ('row', 'col'), split_axis=0, concat_axis=0, til...]
    scatter x1 -> x0, local copies, waits for them, and re-layouts: 52.9 us -> none  [shards(): old_of_new = jnp.zeros((unknowns,), jnp.int32).at[new_index].set(places)]
    dot_general x1 -> x0, matrix products: 25.2 us -> none  [shards(): jnp.dot(tile_layout, check_vectors, precision=lax.Precision.HIGHEST, pref...]
    select_n x5 -> x1, other arithmetic: 24.9 us -> 1.68 us  [shards(): jnp.where(place < keep, block * keep + place, devices * keep + block * 8...]
  transfers between devices with their start and end apart: 2 -> 2, of which waited for: 2 -> 2; matrix products, arithmetic and copies ran while one was open for 13% -> 0% of each run, Pallas kernels for 0% -> 0%
where the time goes in v1:
time: 314 us
  blocking collectives  142 us (45%)
  waiting for transfers between devices  80.1 us (26%)
  Pallas kernels  78.7 us (25%)
  other arithmetic  7.7 us (2%)
  starting transfers between devices  4.76 us (2%)
    all_to_all x1, blocking collectives, shards(): lax.all_to_all(outgoing, ('row', 'col'), split_axis=0, concat_axis=0, til...  91.6 us
    all_to_all x1, waiting for transfers between devices, shards(): lax.all_to_all(chosen, 'row', split_axis=0, concat_axis=0, tiled=True)  73.5 us
    all_to_all x1, blocking collectives, shards(): lax.all_to_all(both, 'col', split_axis=0, concat_axis=0, axis_index_group...  50 us
    pallas_call x1, Pallas kernels, group_columns(): pl.pallas_call(kernel, grid_spec=pltpu.PrefetchScalarGridSpec(num_scalar_...  31.2 us
    pallas_call x1, Pallas kernels, group_rows(): pl.pallas_call(kernel, grid_spec=pltpu.PrefetchScalarGridSpec(num_scalar_...  26.5 us
    pallas_call x1, Pallas kernels, tile_and_product(): pl.pallas_call(kernel, grid_spec=pltpu.PrefetchScalarGridSpec(num_scalar_...  21.1 us
    ppermute x1, waiting for transfers between devices, shards(): both = mine + lax.ppermute(other, 'col', swap)  6.62 us
  transfers between devices with their start and end apart: 2, of which 2 were waited for; matrix products, arithmetic and copies ran while one was open for 0% of the time, Pallas kernels for 0%

profile of v1, /device:TPU:0, one launch (start us, length us, event | category | flops | bytes accessed | tf_op | source)
XLA Modules:
  0.0 313.6 jit_solution(10724718517344735581)
XLA Ops:
  0.6 1.7 add_select_fusion.8
  2.3 31.2 %group_columns.1 = f32[128,104,128]{2,1,0:T(8,128)} custom-call(s32[14336]{0:T(1024)} %get-tuple-element.8.pos_ref, f32[112,14336]{1,0:T(8,128)} %x_ref.1), custom_call_target="tpu_custom_call" | custom-call | tf_op jit(solution)/shard_map/group_columns/pallas_call | solution.py:47
  33.5 91.6 %all_to_all.15.x_ref = f32[128,104,128]{2,1,0:T(8,128)} all-to-all(f32[128,104,128]{2,1,0:T(8,128)} %group_columns.1), channel_id=1, replica_groups=mesh['row'=8,'col'=16] {'row','col'}, dimensions={0} | all-to-all | bytes 13631488 | tf_op jit(solution)/shard_map/all_to_all | solution.py:181
  125.1 26.5 %group_rows.1 = f32[8,112,1792]{2,1,0:T(8,128)} custom-call(s32[14336]{0:T(1024)} %get-tuple-element.9.pos_ref, f32[128,104,128]{2,1,0:T(8,128)} %all_to_all.15.x_ref), custom_call_target="tpu_custom_call" | custom-call | tf_op jit(solution)/shard_map/group_rows/pallas_call | solution.py:92
  151.6 4.8 %all-to-all-start.1 = ((f32[8,112,1792]{2,1,0:T(8,128)}), f32[8,112,1792]{2,1,0:T(8,128)}, u32[]{:S(2)}, u32[]{:S(2)}) async-start(f32[8,112,1792]{2,1,0:T(8,128)} %group_rows.1), calls=%async_computation.1 | async-start | bytes 12845056 | tf_op jit(solution)/shard_map/all_to_all | solution.py:183
  156.4 73.5 %all-to-all-done.1 = f32[8,112,1792]{2,1,0:T(8,128)} async-done(((f32[8,112,1792]{2,1,0:T(8,128)}), f32[8,112,1792]{2,1,0:T(8,128)}, u32[]{:S(2)}, u32[]{:S(2)}) %all-to-all-start.1) | async-done | bytes 6422560 | tf_op jit(solution)/shard_map/all_to_all | solution.py:183
  229.8 21.1 %tile_and_product.1 = (f32[1792,896]{1,0:T(8,128)}, f32[8,112,1024]{2,1,0:T(8,128)}, f32[8,112,1024]{2,1,0:T(8,128)}) custom-call(s32[1]{0:T(128)} %bitcast.core_ref, f32[896,1792]{1,0:T(8,128)} %bitcast.1.x_ref, f32[896,1024]{1,0:T(8,128)} %v_ref.1), custom_call_target="tpu_custom_call" | custom-call | tf_op jit(solution)/shard_map/tile_and_product/pallas_call | solution.py:143
  250.9 0.0 collective-permute-start
  250.9 6.6 %collective-permute-done = f32[8,112,1024]{2,1,0:T(8,128)S(1)} collective-permute-done((f32[8,112,1024]{2,1,0:T(8,128)}, f32[8,112,1024]{2,1,0:T(8,128)S(1)}, u32[]{:S(2)}, u32[]{:S(2)}) %collective-permute-start) | collective-permute-done | bytes 3670048 | tf_op jit(solution)/shard_map/ppermute | solution.py:190
  257.5 2.9 add.67
  260.4 50.0 %all_to_all.16 = f32[8,112,1024]{2,1,0:T(8,128)} all-to-all(f32[8,112,1024]{2,1,0:T(8,128)S(1)} %add.67), channel_id=1, replica_groups={{0,2,4,6,8,10,12,14},{1,3,5,7,9,11,13,15},{16,18,20,22,24,26,28,30},{17..., dimensions={0} | all-to-all | bytes 7340032 | tf_op jit(solution)/shard_map/all_to_all | solution.py:192
  310.4 3.2 %reduce_sum.9 = f32[112,1024]{1,0:T(8,128)} reduce(f32[8,112,1024]{2,1,0:T(8,128)} %all_to_all.16, f32[]{:T(128)} %constant.106.clone.1), dimensions={0}, to_apply=%region_0.1 | reduce | flops 802816 | bytes 4128772 | tf_op jit(solution)/shard_map/reduce_sum | solution.py:193
Async XLA Ops:
  151.6 78.2 %all-to-all-start.1 = ((f32[8,112,1792]{2,1,0:T(8,128)}), f32[8,112,1792]{2,1,0:T(8,128)}, u32[]{:S(2)}, u32[]{:S(2)}) async-start(f32[8,112,1792]{2,1,0:T(8,128)} %group_rows.1), calls=%async_computation.1 | async-start | bytes 12845056 | tf_op jit(solution)/shard_map/all_to_all | solution.py:183
  250.9 6.6 %collective-permute-start = (f32[8,112,1024]{2,1,0:T(8,128)}, f32[8,112,1024]{2,1,0:T(8,128)S(1)}, u32[]{:S(2)}, u32[]{:S(2)}) collective-permute-start(f32[8,112,1024]{2,1,0:T(8,128)} %get-tuple-element.7), channel_id=1, source_target_pairs={{0,1},{1,0},{2,3},{3,2},{4,5},{5,4},{6,7},{7,6},{8,9},{9,8},{10,11... | collective-permute-start | bytes 11010056 | tf_op jit(solution)/shard_map/ppermute | solution.py:190

commit v2 on v0

v2 whole, which is shorter than its diff:
```python
import jax
import jax.numpy as jnp
from jax import lax
from jax.experimental import pallas as pl
from jax.experimental.pallas import tpu as pltpu
from jax.sharding import PartitionSpec as P

TILE = 128
LANES = 128
SUB = 8
VMEM = 56 * 1024 * 1024


def scatter_rows(pos_ref, base, src_ref, dst_ref, count, unroll=32):
    def body(i, carry):
        start = i * unroll
        for u in range(unroll):
            dst_ref[pl.ds(pos_ref[base + start + u], 1), :] = src_ref[pl.ds(start + u, 1), :]
        return carry

    lax.fori_loop(0, count // unroll, body, 0)


def params(**kwargs):
    return pltpu.CompilerParams(vmem_limit_bytes=VMEM, **kwargs)


def group_columns(slab, places, devices, full, rest):
    share, unknowns = slab.shape
    steps = 4
    width = unknowns // steps
    keep = full - SUB
    chunk = LANES - share
    outs = 4
    per = devices // outs
    second = devices * keep
    extra_at = second + devices * rest

    def kernel(pos_ref, x_ref, full_ref, rest_ref, turned, spread):
        step = pl.program_id(0)

        @pl.when(step < steps)
        def _():
            for b in range(width // LANES):
                turned[b * LANES:(b + 1) * LANES, :share] = x_ref[:, b * LANES:(b + 1) * LANES].T
            scatter_rows(pos_ref, step * width, turned, spread, width)

        @pl.when(step >= steps)
        def _():
            first = (step - steps) * per

            def pack(i, carry):
                for u in range(8):
                    b = i * 8 + u
                    d = first + b
                    full_ref[b] = spread[pl.ds(pl.multiple_of(d * keep, SUB), keep), :]
                    rest_ref[b] = spread[pl.ds(pl.multiple_of(second + d * rest, SUB), rest), :]
                    extra = spread[pl.ds(pl.multiple_of(extra_at + d * SUB, SUB), SUB), :]
                    for k in range(share // chunk):
                        full_ref[b, SUB * k:SUB * k + SUB, share:] = extra[:, chunk * k:chunk * (k + 1)]
                return carry

            lax.fori_loop(0, per // 8, pack, 0)

    late = lambda g, pos: (jnp.maximum(g - steps, 0), 0, 0)
    return pl.pallas_call(
        kernel,
        grid_spec=pltpu.PrefetchScalarGridSpec(
            num_scalar_prefetch=1,
            grid=(steps + outs,),
            in_specs=[pl.BlockSpec((share, width), lambda g, pos: (0, jnp.minimum(g, steps - 1)))],
            out_specs=[
                pl.BlockSpec((per, keep, LANES), late),
                pl.BlockSpec((per, rest, LANES), late),
            ],
            scratch_shapes=[
                pltpu.VMEM((width, LANES), jnp.float32),
                pltpu.VMEM((unknowns, LANES), jnp.float32),
            ],
        ),
        out_shape=[
            jax.ShapeDtypeStruct((devices, keep, LANES), jnp.float32),
            jax.ShapeDtypeStruct((devices, rest, LANES), jnp.float32),
        ],
        compiler_params=params(),
        name="group_columns",
    )(places, slab)


def group_rows(blocks, places, groups, share, packed, widths, label):
    devices, held, _ = blocks.shape
    count = held + SUB if packed else held
    unknowns = devices * share
    chunk = LANES - share
    steps = 4
    per = devices // steps
    rows = unknowns // groups
    starts = [sum(widths[:i]) for i in range(len(widths))]
    outs = groups

    def kernel(pos_ref, x_ref, *refs):
        out_refs, (turned, spread) = refs[:-2], refs[-2:]
        step = pl.program_id(0)

        @pl.when(step < steps)
        def _():
            def flip(i, carry):
                for u in range(4):
                    b = i * 4 + u
                    flipped = x_ref[b].T
                    at = pl.multiple_of(b * share, SUB)
                    turned[pl.ds(at, share), :held] = flipped[:share]
                    if packed:
                        for k in range(share // chunk):
                            turned[pl.ds(at + k * chunk, chunk), held:count] = flipped[share:, SUB * k:SUB * k + SUB]
                return carry

            lax.fori_loop(0, per // 4, flip, 0)
            scatter_rows(pos_ref, step * per * share, turned, spread, per * share)

        @pl.when(step >= steps)
        def _():
            g = step - steps
            for ref, start, width in zip(out_refs, starts, widths):
                for k in range(width // LANES):
                    at = pl.multiple_of(g * rows + start + k * LANES, LANES)
                    ref[0, :, k * LANES:(k + 1) * LANES] = spread[pl.ds(at, LANES), :].T[:count]

    late = lambda g, pos: (jnp.maximum(g - steps, 0), 0, 0)
    return pl.pallas_call(
        kernel,
        grid_spec=pltpu.PrefetchScalarGridSpec(
            num_scalar_prefetch=1,
            grid=(steps + outs,),
            in_specs=[pl.BlockSpec((per, held, LANES), lambda g, pos: (jnp.minimum(g, steps - 1), 0, 0))],
            out_specs=[pl.BlockSpec((1, count, w), late) for w in widths],
            scratch_shapes=[
                pltpu.VMEM((per * share, LANES), jnp.float32),
                pltpu.VMEM((unknowns, LANES), jnp.float32),
            ],
        ),
        out_shape=[jax.ShapeDtypeStruct((groups, count, w), jnp.float32) for w in widths],
        compiler_params=params(),
        cost_estimate=pl.CostEstimate(flops=20_000_000_000, bytes_accessed=2 * unknowns * count * 4, transcendentals=0),
        name=label,
    )(places, blocks)


def tile_and_product(pieces, v_hi, v_lo, core, tile, cols, share, index, label):
    groups, _, rows = pieces[0].shape
    counts = [p.shape[1] for p in pieces]
    span = rows // cols
    columns, width = v_hi.shape
    steps = 4
    wide = width // steps

    def kernel(core_ref, *refs):
        x_refs = refs[:len(pieces)]
        hi_ref, lo_ref = refs[len(pieces):len(pieces) + 2]
        tile_ref, other_ref, mine_ref, x_hi, x_lo = refs[-5:]
        step = pl.program_id(0)

        @pl.when(step == 0)
        def _():
            for k in range(rows // LANES):
                held = []
                for g in range(groups):
                    for x_ref in x_refs:
                        held.append(x_ref[g, :, k * LANES:(k + 1) * LANES])
                x = jnp.concatenate(held, axis=0).T
                hi = x.astype(jnp.bfloat16)
                x_hi[k * LANES:(k + 1) * LANES, :] = hi
                x_lo[k * LANES:(k + 1) * LANES, :] = (x - hi.astype(jnp.float32)).astype(jnp.bfloat16)
                for s in range(0, LANES, SUB):
                    c, m = divmod(k * LANES + s, span)
                    tile_ref[c, m:m + SUB, :] = x[s:s + SUB]

        part = (
            jnp.dot(x_hi[...], hi_ref[...], preferred_element_type=jnp.float32)
            + jnp.dot(x_hi[...], lo_ref[...], preferred_element_type=jnp.float32)
            + jnp.dot(x_lo[...], hi_ref[...], preferred_element_type=jnp.float32)
        )
        even = core_ref[0] == 0
        for c in range(cols // 2):
            first = part[2 * c * span:(2 * c + 1) * span]
            second = part[(2 * c + 1) * span:(2 * c + 2) * span]
            other_ref[c] = jnp.where(even, second, first)
            mine_ref[c] = jnp.where(even, first, second)

    half = jax.ShapeDtypeStruct((cols // 2, span, width), jnp.float32)
    half_spec = pl.BlockSpec((cols // 2, span, wide), lambda g, core: (0, 0, g))
    in_specs = [pl.BlockSpec((groups, n, rows), lambda g, core: (0, 0, 0)) for n in counts]
    in_specs += [pl.BlockSpec((columns, wide), lambda g, core: (0, g))] * 2
    operands = [core, *pieces, v_hi, v_lo]
    aliases = {}
    if tile is not None:
        aliases = {len(operands): 0}
        operands.append(tile)
        in_specs.append(pl.BlockSpec(memory_space=pl.ANY))
    return pl.pallas_call(
        kernel,
        grid_spec=pltpu.PrefetchScalarGridSpec(
            num_scalar_prefetch=1,
            grid=(steps,),
            in_specs=in_specs,
            out_specs=[pl.BlockSpec((cols, span, columns), lambda g, core: (0, index, 0)), half_spec, half_spec],
            scratch_shapes=[
                pltpu.VMEM((rows, columns), jnp.bfloat16),
                pltpu.VMEM((rows, columns), jnp.bfloat16),
            ],
        ),
        out_shape=[jax.ShapeDtypeStruct((cols, share, columns), jnp.float32), half, half],
        input_output_aliases=aliases,
        compiler_params=params(),
        cost_estimate=pl.CostEstimate(flops=6 * rows * columns * width, bytes_accessed=8 * rows * columns, transcendentals=0),
        name=label,
    )(*operands)


def shards(normal_matrix, new_index, check_vectors):
    row_count = lax.axis_size("row")
    col_count = lax.axis_size("col")
    devices = row_count * col_count
    share, unknowns = normal_matrix.shape
    full, rest = 64, 48
    spans = (56, 56)
    keep = full - SUB
    rows = unknowns // row_count

    tile, lane = new_index // TILE, new_index % TILE
    within_col = tile // col_count * TILE + lane
    block = within_col // share * col_count + tile % col_count
    place = within_col % share
    column_places = jnp.where(
        place < keep,
        block * keep + place,
        jnp.where(
            place < full,
            devices * (keep + rest) + block * SUB + place - keep,
            devices * keep + block * rest + place - full,
        ),
    )
    within_row = tile // row_count * TILE + lane
    owner, m = within_row // share, within_row % share
    spot = jnp.zeros_like(m)
    start = 0
    for span in spans:
        spot = jnp.where((m >= start) & (m < start + span), start * col_count + owner * span + m - start, spot)
        start += span
    row_places = tile % row_count * rows + spot

    exchange = lambda x: lax.all_to_all(x, ("row", "col"), split_axis=0, concat_axis=0, tiled=True)
    along = lambda x: lax.all_to_all(x, "row", split_axis=0, concat_axis=0, tiled=True)
    groups = [list(range(p, col_count, 2)) for p in range(2)]
    swap = [(i, i ^ 1) for i in range(col_count)]
    widths = [s * col_count for s in spans]

    out_full, out_rest = group_columns(normal_matrix, column_places, devices, full, rest)
    in_full = exchange(out_full)
    out_rest, in_full = lax.optimization_barrier((out_rest, in_full))
    in_rest = exchange(out_rest)
    v_hi = lax.reduce_precision(check_vectors, 8, 7)
    v_lo = (check_vectors - v_hi).astype(jnp.bfloat16)
    v_hi = v_hi.astype(jnp.bfloat16)
    core = (lax.axis_index("col") % 2).astype(jnp.int32).reshape(1)

    chosen_full = group_rows(in_full, row_places, row_count, share, True, widths, "group_rows_full")
    chosen_rest = group_rows(in_rest, row_places, row_count, share, False, widths, "group_rows_rest")

    tile_layout = None
    sums = []
    last = in_rest
    for q, span in enumerate(spans):
        pieces = []
        for chosen in (chosen_full, chosen_rest):
            send, _ = lax.optimization_barrier((chosen[q], last))
            last = along(send)
            pieces.append(last)
        tile_layout, other, mine = tile_and_product(
            pieces, v_hi, v_lo, core, tile_layout, col_count, share, q, f"tile_and_product_{q}"
        )
        both = mine + lax.ppermute(other, "col", swap)
        parts = lax.all_to_all(both, "col", split_axis=0, concat_axis=0, axis_index_groups=groups, tiled=True)
        sums.append(parts.sum(axis=0))
    return tile_layout.reshape(rows, unknowns // col_count), jnp.concatenate(sums, axis=0)


def solution(mesh):
    return jax.shard_map(
        shards,
        mesh=mesh,
        in_specs=(P(("row", "col"), None), P(), P("col", None)),
        out_specs=(P("row", "col"), P(("row", "col"), None)),
        check_vma=False,
    )
```

time: 606 us -> 312 us (0.51)
  local copies, waits for them, and re-layouts: 348 us -> 2.77 us
  Pallas kernels: 0 us -> 98.8 us
  matrix products: 25.2 us -> 0 us
  starting transfers between devices: 11.7 us -> 26.5 us
  between operations: 14.1 us -> 0.73 us
  waiting for transfers between devices: 98.4 us -> 85.3 us
  other arithmetic: 25 us -> 14.4 us
    gather x4 -> x0, local copies, waits for them, and re-layouts: 261 us -> none  [the longest x1 79.3 us: shards(): old_of_new[new_of_packed(places, row_count, unknowns // row_count, TILE)]]
    pallas_call x0 -> x5, Pallas kernels: none -> 98.8 us  [the longest x2 52.8 us: group_rows(): pl.pallas_call(kernel, grid_spec=pltpu.PrefetchScalarGridSpec(num_scalar_...]
    reduce_scatter x1 -> x0, waiting for transfers between devices: 89.6 us -> none  [shards(): lax.psum_scatter(jnp.dot(tile_layout, check_vectors, precision=lax.Precis...]
    all_to_all x1 -> x6, waiting for transfers between devices: 8.8 us -> 85.2 us  [the longest x2 47.9 us: shards(): lax.all_to_all(both, 'col', split_axis=0, concat_axis=0, axis_index_group...]
    scatter x1 -> x0, local copies, waits for them, and re-layouts: 52.9 us -> none  [shards(): old_of_new = jnp.zeros((unknowns,), jnp.int32).at[new_index].set(places)]
    dot_general x1 -> x0, matrix products: 25.2 us -> none  [shards(): jnp.dot(tile_layout, check_vectors, precision=lax.Precision.HIGHEST, pref...]
    select_n x5 -> x1, other arithmetic: 24.9 us -> 1.77 us  [shards(): jnp.where(place < keep, block * keep + place, jnp.where(place < full, dev...]
    all_to_all x2 -> x0, local copies, waits for them, and re-layouts: 16.9 us -> none  [the longest x1 8.62 us: shards(): lax.all_to_all(outgoing, ('row', 'col'), split_axis=0, concat_axis=0, til...]
  transfers between devices with their start and end apart: 2 -> 8, of which waited for: 2 -> 5; matrix products, arithmetic and copies ran while one was open for 13% -> 3% of each run, Pallas kernels for 0% -> 25%
where the time goes in v2:
time: 312 us; the launch traced here: 311 us
  Pallas kernels  98.8 us (32%)
  waiting for transfers between devices  85.3 us (27%)
  blocking collectives  82.6 us (26%)
  starting transfers between devices  26.5 us (8%)
  other arithmetic  14.4 us (5%)
    all_to_all x1, blocking collectives, shards(): lax.all_to_all(x, ('row', 'col'), split_axis=0, concat_axis=0, tiled=True)  57.7 us
    pallas_call x2, Pallas kernels, group_rows(): pl.pallas_call(kernel, grid_spec=pltpu.PrefetchScalarGridSpec(num_scalar_...  52.8 us
    all_to_all x2, waiting for transfers between devices, shards(): lax.all_to_all(both, 'col', split_axis=0, concat_axis=0, axis_index_group...  47.9 us
    all_to_all x1, blocking collectives, shards(): lax.all_to_all(x, 'row', split_axis=0, concat_axis=0, tiled=True)  24.9 us
    all_to_all x3, waiting for transfers between devices, shards(): lax.all_to_all(x, 'row', split_axis=0, concat_axis=0, tiled=True)  24.8 us
    pallas_call x2, Pallas kernels, tile_and_product(): pl.pallas_call(kernel, grid_spec=pltpu.PrefetchScalarGridSpec(num_scalar_...  23.4 us
    pallas_call x1, Pallas kernels, group_columns(): pl.pallas_call(kernel, grid_spec=pltpu.PrefetchScalarGridSpec(num_scalar_...  22.5 us
    all_to_all x1, waiting for transfers between devices, shards(): lax.all_to_all(x, ('row', 'col'), split_axis=0, concat_axis=0, tiled=True)  12.5 us
  transfers between devices with their start and end apart: 8, of which 5 were waited for; matrix products, arithmetic and copies ran while one was open for 3% of the time, Pallas kernels for 25%

profile of v2, /device:TPU:0, one launch (start us, length us, event | category | flops | bytes accessed | tf_op | source)
XLA Modules:
  0.0 311.0 jit_solution(5496037930572150709)
XLA Ops:
  0.6 1.8 select_select_fusion
  2.4 22.5 %group_columns.1 = (f32[128,56,128]{2,1,0:T(8,128)}, f32[128,48,128]{2,1,0:T(8,128)}) custom-call(s32[14336]{0:T(1024)} %get-tuple-element.40.pos_ref, f32[112,14336]{1,0:T(8,128)} %x_ref.1), custom_call_target="tpu_custom_call" | custom-call | tf_op jit(solution)/shard_map/group_columns/pallas_call | solution.py:66
  24.9 57.7 %all_to_all.40.x_ref = f32[128,56,128]{2,1,0:T(8,128)} all-to-all(f32[128,56,128]{2,1,0:T(8,128)} %get-tuple-element.21), channel_id=1, replica_groups=mesh['row'=8,'col'=16] {'row','col'}, dimensions={0} | all-to-all | bytes 7340032 | tf_op jit(solution)/shard_map/all_to_all | solution.py:252
  82.7 6.2 %all-to-all-start.1 = ((f32[128,48,128]{2,1,0:T(8,128)}), f32[128,48,128]{2,1,0:T(8,128)S(1)}, u32[]{:S(2)}, u32[]{:S(2)}) async-start(f32[128,48,128]{2,1,0:T(8,128)} %get-tuple-element.24), calls=%async_computation.1 | async-start | bytes 6291456 | tf_op jit(solution)/shard_map/all_to_all | solution.py:252
  88.8 28.3 %group_rows_full.1 = (f32[8,64,896]{2,1,0:T(8,128)}, f32[8,64,896]{2,1,0:T(8,128)}) custom-call(s32[14336]{0:T(1024)} %get-tuple-element.41.pos_ref, f32[128,56,128]{2,1,0:T(8,128)} %all_to_all.40.x_ref), custom_call_target="tpu_custom_call" | custom-call | flops 20000000000 | bytes 7340032 | tf_op jit(solution)/shard_map/group_rows_full/pallas_call | solution.py:130
  117.1 12.5 %all-to-all-done.1.x_ref = f32[128,48,128]{2,1,0:T(8,128)S(1)} async-done(((f32[128,48,128]{2,1,0:T(8,128)}), f32[128,48,128]{2,1,0:T(8,128)S(1)}, u32[]{:S(2)}, u32[]{:S(2)}) %all-to-all-start.1) | async-done | bytes 3145760 | tf_op jit(solution)/shard_map/all_to_all | solution.py:252
  129.6 0.0 copy-start
  129.6 1.7 copy-done
  131.3 4.3 %all-to-all-start.2 = ((f32[8,64,896]{2,1,0:T(8,128)}), f32[8,64,896]{2,1,0:T(8,128)}, u32[]{:S(2)}, u32[]{:S(2)}) async-start(f32[8,64,896]{2,1,0:T(8,128)} %get-tuple-element.27), calls=%async_computation.2 | async-start | bytes 3670016 | tf_op jit(solution)/shard_map/all_to_all | solution.py:253
  135.6 24.5 %group_rows_rest.1 = (f32[8,48,896]{2,1,0:T(8,128)}, f32[8,48,896]{2,1,0:T(8,128)}) custom-call(s32[14336]{0:T(1024)} %get-tuple-element.41.pos_ref, f32[128,48,128]{2,1,0:T(8,128)} %copy-done), custom_call_target="tpu_custom_call" | custom-call | flops 20000000000 | bytes 5505024 | tf_op jit(solution)/shard_map/group_rows_rest/pallas_call | solution.py:130
  160.1 0.0 all-to-all-done.2.refs_0_
  160.1 24.9 %all_to_all.41.refs_1_ = f32[8,48,896]{2,1,0:T(8,128)} all-to-all(f32[8,48,896]{2,1,0:T(8,128)} %get-tuple-element.28), channel_id=1, replica_groups=mesh['row'=8,'col'=16] {'row'}, dimensions={0} | all-to-all | bytes 2752512 | tf_op jit(solution)/shard_map/all_to_all | solution.py:253
  185.0 3.6 %all-to-all-start.4 = ((f32[8,64,896]{2,1,0:T(8,128)}), f32[8,64,896]{2,1,0:T(8,128)S(1)}, u32[]{:S(2)}, u32[]{:S(2)}) async-start(f32[8,64,896]{2,1,0:T(8,128)} %get-tuple-element.29), calls=%async_computation.4 | async-start | bytes 3670016 | tf_op jit(solution)/shard_map/all_to_all | solution.py:253
  188.6 4.7 %fusion = (bf16[896,1024]{1,0:T(8,128)(2,1)}, bf16[896,1024]{1,0:T(8,128)(2,1)}) fusion(f32[896,1024]{1,0:T(8,128)} %param.5), kind=kLoop, calls=%fused_computation.2 | loop fusion | flops 3670016 | bytes 7340032 | tf_op jit(solution)/shard_map/convert_element_type | solution.py:263
  193.4 18.1 %all-to-all-done.4.refs_0_ = f32[8,64,896]{2,1,0:T(8,128)S(1)} async-done(((f32[8,64,896]{2,1,0:T(8,128)}), f32[8,64,896]{2,1,0:T(8,128)S(1)}, u32[]{:S(2)}, u32[]{:S(2)}) %all-to-all-start.4) | async-done | bytes 1835040 | tf_op jit(solution)/shard_map/all_to_all | solution.py:253
  211.5 0.0 copy-start.1
  211.5 3.6 %all-to-all-start.5 = ((f32[8,48,896]{2,1,0:T(8,128)}), f32[8,48,896]{2,1,0:T(8,128)S(1)}, u32[]{:S(2)}, u32[]{:S(2)}) async-start(f32[8,48,896]{2,1,0:T(8,128)} %get-tuple-element.31), calls=%async_computation.5 | async-start | bytes 2752512 | tf_op jit(solution)/shard_map/all_to_all | solution.py:253
  215.1 11.7 %tile_and_product_0.1 = (f32[16,112,896]{2,1,0:T(8,128)}, f32[8,56,1024]{2,1,0:T(8,128)}, f32[8,56,1024]{2,1,0:T(8,128)}) custom-call(s32[1]{0:T(128)} %bitcast.core_ref, f32[8,64,896]{2,1,0:T(8,128)} %all-to-all-done.2.refs_0_, f32[8,48,896]{2,1,0:T(8,128)} %all_to_all.41.refs_1_, bf16[896,1024]{1,0:T(8,128)(2,1)} %get-tuple-element.39.refs_2_, ...), custom_call_target="tpu_custom_call" | custom-call | flops 4932501504 | bytes 6422528 | tf_op jit(solution)/shard_map/tile_and_product_0/pallas_call | solution.py:200
  226.7 0.0 copy-done.1
  226.7 0.1 collective-permute-start
  226.8 6.7 %all-to-all-done.5.refs_1_ = f32[8,48,896]{2,1,0:T(8,128)S(1)} async-done(((f32[8,48,896]{2,1,0:T(8,128)}), f32[8,48,896]{2,1,0:T(8,128)S(1)}, u32[]{:S(2)}, u32[]{:S(2)}) %all-to-all-start.5) | async-done | bytes 1376288 | tf_op jit(solution)/shard_map/all_to_all | solution.py:253
  233.5 0.0 copy-start.3
  233.5 1.1 copy-done.3
  234.6 0.0 copy-start.2
  234.6 11.8 %tile_and_product_1.1 = (f32[16,112,896]{2,1,0:T(8,128)}, f32[8,56,1024]{2,1,0:T(8,128)}, f32[8,56,1024]{2,1,0:T(8,128)}) custom-call(s32[1]{0:T(128)} %bitcast.core_ref, f32[8,64,896]{2,1,0:T(8,128)} %copy-done.1, f32[8,48,896]{2,1,0:T(8,128)} %copy-done.3, bf16[896,1024]{1,0:T(8,128)(2,1)} %get-tuple-element.39.refs_2_, ...), custom_call_target="tpu_custom_call", output_to_operand_aliasing={{0}: (5, {})} | custom-call | flops 4932501504 | bytes 6422528 | tf_op jit(solution)/shard_map/tile_and_product_1/pallas_call | solution.py:200
  246.4 0.0 collective-permute-start.1
  246.4 0.0 collective-permute-done
  246.4 0.0 copy-done.2
  246.4 1.6 add.106
  248.0 4.5 %all-to-all-start.6 = ((f32[8,56,1024]{2,1,0:T(8,128)}), f32[8,56,1024]{2,1,0:T(8,128)S(1)}, u32[]{:S(2)}, u32[]{:S(2)}) async-start(f32[8,56,1024]{2,1,0:T(8,128)} %add.106), calls=%async_computation.6 | async-start | bytes 3670016 | tf_op jit(solution)/shard_map/all_to_all | solution.py:283
  252.5 0.0 collective-permute-done.1
  252.5 3.7 %add.107 = f32[8,56,1024]{2,1,0:T(8,128)} add(f32[8,56,1024]{2,1,0:T(8,128)} %get-tuple-element.36, f32[8,56,1024]{2,1,0:T(8,128)} %collective-permute-done.1) | non-fusion elementwise | flops 458752 | bytes 5505024 | tf_op jit(solution)/shard_map/add | solution.py:282
  256.2 22.6 %all-to-all-done.6 = f32[8,56,1024]{2,1,0:T(8,128)S(1)} async-done(((f32[8,56,1024]{2,1,0:T(8,128)}), f32[8,56,1024]{2,1,0:T(8,128)S(1)}, u32[]{:S(2)}, u32[]{:S(2)}) %all-to-all-start.6) | async-done | bytes 1835040 | tf_op jit(solution)/shard_map/all_to_all | solution.py:283
  278.8 4.3 %all-to-all-start.7 = ((f32[8,56,1024]{2,1,0:T(8,128)}), f32[8,56,1024]{2,1,0:T(8,128)}, u32[]{:S(2)}, u32[]{:S(2)}) async-start(f32[8,56,1024]{2,1,0:T(8,128)} %add.107), calls=%async_computation.7 | async-start | bytes 3670016 | tf_op jit(solution)/shard_map/all_to_all | solution.py:283
  283.1 0.1 reduce_sum.18
  283.2 25.3 %all-to-all-done.7 = f32[8,56,1024]{2,1,0:T(8,128)} async-done(((f32[8,56,1024]{2,1,0:T(8,128)}), f32[8,56,1024]{2,1,0:T(8,128)}, u32[]{:S(2)}, u32[]{:S(2)}) %all-to-all-start.7) | async-done | bytes 1835040 | tf_op jit(solution)/shard_map/all_to_all | solution.py:283
  308.6 1.6 reduce_sum.19
  310.2 0.8 pad_maximum_fusion
Async XLA Ops:
  82.7 47.0 %all-to-all-start.1 = ((f32[128,48,128]{2,1,0:T(8,128)}), f32[128,48,128]{2,1,0:T(8,128)S(1)}, u32[]{:S(2)}, u32[]{:S(2)}) async-start(f32[128,48,128]{2,1,0:T(8,128)} %get-tuple-element.24), calls=%async_computation.1 | async-start | bytes 6291456 | tf_op jit(solution)/shard_map/all_to_all | solution.py:252
  129.6 1.7 copy-start
  131.3 28.9 %all-to-all-start.2 = ((f32[8,64,896]{2,1,0:T(8,128)}), f32[8,64,896]{2,1,0:T(8,128)}, u32[]{:S(2)}, u32[]{:S(2)}) async-start(f32[8,64,896]{2,1,0:T(8,128)} %get-tuple-element.27), calls=%async_computation.2 | async-start | bytes 3670016 | tf_op jit(solution)/shard_map/all_to_all | solution.py:253
  185.0 26.4 %all-to-all-start.4 = ((f32[8,64,896]{2,1,0:T(8,128)}), f32[8,64,896]{2,1,0:T(8,128)S(1)}, u32[]{:S(2)}, u32[]{:S(2)}) async-start(f32[8,64,896]{2,1,0:T(8,128)} %get-tuple-element.29), calls=%async_computation.4 | async-start | bytes 3670016 | tf_op jit(solution)/shard_map/all_to_all | solution.py:253
  211.5 15.2 %copy-start.1 = (f32[8,64,896]{2,1,0:T(8,128)}, f32[8,64,896]{2,1,0:T(8,128)S(1)}, u32[]{:S(2)}) copy-start(f32[8,64,896]{2,1,0:T(8,128)S(1)} %all-to-all-done.4.refs_0_) | copy-start | bytes 5505028
  211.5 22.0 %all-to-all-start.5 = ((f32[8,48,896]{2,1,0:T(8,128)}), f32[8,48,896]{2,1,0:T(8,128)S(1)}, u32[]{:S(2)}, u32[]{:S(2)}) async-start(f32[8,48,896]{2,1,0:T(8,128)} %get-tuple-element.31), calls=%async_computation.5 | async-start | bytes 2752512 | tf_op jit(solution)/shard_map/all_to_all | solution.py:253
  226.7 19.7 %collective-permute-start = (f32[8,56,1024]{2,1,0:T(8,128)}, f32[8,56,1024]{2,1,0:T(8,128)S(1)}, u32[]{:S(2)}, u32[]{:S(2)}) collective-permute-start(f32[8,56,1024]{2,1,0:T(8,128)} %get-tuple-element.35), channel_id=1, source_target_pairs={{0,1},{1,0},{2,3},{3,2},{4,5},{5,4},{6,7},{7,6},{8,9},{9,8},{10,11... | collective-permute-start | bytes 5505032 | tf_op jit(solution)/shard_map/ppermute | solution.py:282
  233.5 1.1 copy-start.3
  234.6 11.8 %copy-start.2 = (f32[8,56,1024]{2,1,0:T(8,128)S(1)}, f32[8,56,1024]{2,1,0:T(8,128)}, u32[]{:S(2)}) copy-start(f32[8,56,1024]{2,1,0:T(8,128)} %get-tuple-element.34) | copy-start | bytes 5505028
  246.4 6.1 %collective-permute-start.1 = (f32[8,56,1024]{2,1,0:T(8,128)}, f32[8,56,1024]{2,1,0:T(8,128)}, u32[]{:S(2)}, u32[]{:S(2)}) collective-permute-start(f32[8,56,1024]{2,1,0:T(8,128)} %get-tuple-element.37), channel_id=1, source_target_pairs={{0,1},{1,0},{2,3},{3,2},{4,5},{5,4},{6,7},{7,6},{8,9},{9,8},{10,11... | collective-permute-start | bytes 5505032 | tf_op jit(solution)/shard_map/ppermute | solution.py:282
  248.0 30.8 %all-to-all-start.6 = ((f32[8,56,1024]{2,1,0:T(8,128)}), f32[8,56,1024]{2,1,0:T(8,128)S(1)}, u32[]{:S(2)}, u32[]{:S(2)}) async-start(f32[8,56,1024]{2,1,0:T(8,128)} %add.106), calls=%async_computation.6 | async-start | bytes 3670016 | tf_op jit(solution)/shard_map/all_to_all | solution.py:283
  278.8 29.8 %all-to-all-start.7 = ((f32[8,56,1024]{2,1,0:T(8,128)}), f32[8,56,1024]{2,1,0:T(8,128)}, u32[]{:S(2)}, u32[]{:S(2)}) async-start(f32[8,56,1024]{2,1,0:T(8,128)} %add.107), calls=%async_computation.7 | async-start | bytes 3670016 | tf_op jit(solution)/shard_map/all_to_all | solution.py:283

commit v3 on v0

v3 whole, which is shorter than its diff:
```python
import jax
import jax.numpy as jnp
from jax import lax
from jax.experimental import pallas as pl
from jax.experimental.pallas import tpu as pltpu
from jax.sharding import PartitionSpec as P


TILE = 128
LANES = 128
SUB = 8
VMEM = 56 * 1024 * 1024
UNROLL = 32
SPANS = (56, 56)


def params():
    return pltpu.CompilerParams(vmem_limit_bytes=VMEM)


def group_columns(slab, places, devices):
    share, unknowns = slab.shape
    steps, _, width = places.shape
    keep = share - SUB
    chunk = LANES - share
    outs = 4
    per = devices // outs

    def kernel(pos_ref, x_ref, out_ref, turned, spread):
        step = pl.program_id(0)

        @pl.when(step < steps)
        def _():
            for b in range(width // LANES):
                turned[b * LANES:(b + 1) * LANES, :share] = x_ref[:, b * LANES:(b + 1) * LANES].T

            def scatter(i, carry):
                start = i * UNROLL
                for u in range(UNROLL):
                    spread[pl.ds(pos_ref[0, 0, start + u], 1), :] = turned[pl.ds(start + u, 1), :]
                return carry

            lax.fori_loop(0, width // UNROLL, scatter, 0)

        @pl.when(step >= steps)
        def _():
            first = (step - steps) * per

            def pack(i, carry):
                for u in range(8):
                    b = i * 8 + u
                    x = spread[pl.ds(pl.multiple_of((first + b) * share, SUB), share), :].T
                    out_ref[b, :, :share] = x[:keep]
                    for k in range(share // chunk):
                        out_ref[b, SUB * k:SUB * k + SUB, share:] = x[keep:share, chunk * k:chunk * (k + 1)]
                return carry

            lax.fori_loop(0, per // 8, pack, 0)

    return pl.pallas_call(
        kernel,
        grid=(steps + outs,),
        in_specs=[
            pl.BlockSpec((1, 1, width), lambda g: (jnp.minimum(g, steps - 1), 0, 0), memory_space=pltpu.SMEM),
            pl.BlockSpec((share, width), lambda g: (0, jnp.minimum(g, steps - 1))),
        ],
        out_specs=pl.BlockSpec((per, keep, LANES), lambda g: (jnp.maximum(g - steps, 0), 0, 0)),
        scratch_shapes=[
            pltpu.VMEM((width, LANES), jnp.float32),
            pltpu.VMEM((unknowns, LANES), jnp.float32),
        ],
        out_shape=jax.ShapeDtypeStruct((devices, keep, LANES), jnp.float32),
        compiler_params=params(),
        name="group_columns",
    )(places, slab)


def group_rows(blocks, places, groups, share, widths):
    devices, keep, _ = blocks.shape
    unknowns = devices * share
    chunk = LANES - share
    steps = places.shape[0]
    per = devices // steps
    rows = unknowns // groups
    starts = [sum(widths[:i]) for i in range(len(widths))]
    outs = 4
    each = groups // outs

    def kernel(pos_ref, x_ref, *refs):
        out_refs, (extra, spread) = refs[:-2], refs[-2:]
        step = pl.program_id(0)

        @pl.when(step < steps)
        def _():
            def unpack(i, carry):
                for u in range(8):
                    b = i * 8 + u
                    at = pl.multiple_of(b * SUB, SUB)
                    for k in range(share // chunk):
                        extra[pl.ds(at, SUB), chunk * k:chunk * (k + 1)] = x_ref[b, SUB * k:SUB * k + SUB, share:]
                return carry

            lax.fori_loop(0, per // 8, unpack, 0)

            def scatter(b, carry):
                start = b * share
                for u in range(keep):
                    spread[pl.ds(pos_ref[0, 0, start + u], 1), :] = x_ref[b, pl.ds(u, 1), :]
                for u in range(SUB):
                    spread[pl.ds(pos_ref[0, 0, start + keep + u], 1), :] = extra[pl.ds(b * SUB + u, 1), :]
                return carry

            lax.fori_loop(0, per, scatter, 0)

        @pl.when(step >= steps)
        def _():
            def turn(e, carry):
                g = (step - steps) * each + e
                for ref, start, width in zip(out_refs, starts, widths):
                    for k in range(width // LANES):
                        at = pl.multiple_of(g * rows + start + k * LANES, LANES)
                        ref[e, :, k * LANES:(k + 1) * LANES] = spread[pl.ds(at, LANES), :].T[:share]
                return carry

            lax.fori_loop(0, each, turn, 0)

    late = lambda g: (jnp.maximum(g - steps, 0), 0, 0)
    early = lambda g: (jnp.minimum(g, steps - 1), 0, 0)
    return pl.pallas_call(
        kernel,
        grid=(steps + outs,),
        in_specs=[
            pl.BlockSpec((1, 1, per * share), early, memory_space=pltpu.SMEM),
            pl.BlockSpec((per, keep, LANES), early),
        ],
        out_specs=[pl.BlockSpec((each, share, w), late) for w in widths],
        scratch_shapes=[
            pltpu.VMEM((per * SUB, LANES), jnp.float32),
            pltpu.VMEM((unknowns, LANES), jnp.float32),
        ],
        out_shape=[jax.ShapeDtypeStruct((groups, share, w), jnp.float32) for w in widths],
        compiler_params=params(),
        name="group_rows",
    )(places, blocks)


def tile_and_product(turned, v_hi, v_lo, where, tile, cols, share, offset):
    groups, _, rows = turned.shape
    span = rows // cols
    columns, width = v_hi.shape
    steps = 4
    wide = width // steps
    pairs = cols // 2

    def kernel(where_ref, x_ref, hi_ref, lo_ref, *refs):
        tile_ref, other_ref, mine_ref, x_hi, x_lo, held, sem = refs[-7:]
        step = pl.program_id(0)
        store = pltpu.make_async_copy(held, tile_ref.at[:, offset:offset + span, :], sem)

        @pl.when(step == 0)
        def _():
            for k in range(rows // LANES):
                x = x_ref[:, :, k * LANES:(k + 1) * LANES].reshape(columns, LANES).T
                hi = x.astype(jnp.bfloat16)
                x_hi[k * LANES:(k + 1) * LANES, :] = hi
                x_lo[k * LANES:(k + 1) * LANES, :] = (x - hi.astype(jnp.float32)).astype(jnp.bfloat16)
                for s in range(0, LANES, SUB):
                    c, m = divmod(k * LANES + s, span)
                    held[c, m:m + SUB, :] = x[s:s + SUB]
            store.start()

        part = (
            jnp.dot(x_hi[...], hi_ref[...], preferred_element_type=jnp.float32)
            + jnp.dot(x_hi[...], lo_ref[...], preferred_element_type=jnp.float32)
            + jnp.dot(x_lo[...], hi_ref[...], preferred_element_type=jnp.float32)
        )
        even = where_ref[0] == 0
        for c in range(pairs):
            slot = c ^ where_ref[1]
            first = part[2 * c * span:(2 * c + 1) * span]
            second = part[(2 * c + 1) * span:(2 * c + 2) * span]
            other_ref[slot] = jnp.where(even, second, first)
            mine_ref[slot] = jnp.where(even, first, second)

        @pl.when(step == steps - 1)
        def _():
            store.wait()

    half = jax.ShapeDtypeStruct((pairs, span, width), jnp.float32)
    half_spec = pl.BlockSpec((pairs, span, wide), lambda g, where: (0, 0, g))
    in_specs = [pl.BlockSpec((groups, share, rows), lambda g, where: (0, 0, 0))]
    in_specs += [pl.BlockSpec((columns, wide), lambda g, where: (0, g))] * 2
    operands = [where, turned, v_hi, v_lo]
    aliases = {}
    if tile is not None:
        aliases = {len(operands): 0}
        operands.append(tile)
        in_specs.append(pl.BlockSpec(memory_space=pl.ANY))
    return pl.pallas_call(
        kernel,
        grid_spec=pltpu.PrefetchScalarGridSpec(
            num_scalar_prefetch=1,
            grid=(steps,),
            in_specs=in_specs,
            out_specs=[pl.BlockSpec(memory_space=pl.ANY), half_spec, half_spec],
            scratch_shapes=[
                pltpu.VMEM((rows, columns), jnp.bfloat16),
                pltpu.VMEM((rows, columns), jnp.bfloat16),
                pltpu.VMEM((cols, span, columns), jnp.float32),
                pltpu.SemaphoreType.DMA,
            ],
        ),
        out_shape=[jax.ShapeDtypeStruct((cols, share, columns), jnp.float32), half, half],
        input_output_aliases=aliases,
        compiler_params=params(),
        cost_estimate=pl.CostEstimate(flops=6 * rows * columns * width, bytes_accessed=8 * rows * columns, transcendentals=0),
    )(*operands)


def shards(normal_matrix, new_index, check_vectors):
    row_count = lax.axis_size("row")
    col_count = lax.axis_size("col")
    devices = row_count * col_count
    share, unknowns = normal_matrix.shape
    rows = unknowns // row_count
    steps = 4

    tile, lane = new_index // TILE, new_index % TILE
    within_col = tile // col_count * TILE + lane
    column_places = (within_col // share * col_count + tile % col_count) * share + within_col % share
    within_row = tile // row_count * TILE + lane
    owner, m = within_row // share, within_row % share
    spot = jnp.zeros_like(m)
    start = 0
    for span in SPANS:
        spot = jnp.where((m >= start) & (m < start + span), start * col_count + owner * span + m - start, spot)
        start += span
    row_places = tile % row_count * rows + spot
    column_places = column_places.reshape(steps, 1, unknowns // steps)
    row_places = row_places.reshape(steps, 1, unknowns // steps)

    along = lambda x: lax.all_to_all(x, "row", split_axis=0, concat_axis=0, tiled=True)
    flip = lambda x, bits: lax.ppermute(x, "col", [(i, i ^ bits) for i in range(col_count)])
    groups = [list(range(p, col_count, 2)) for p in range(2)]
    widths = [s * col_count for s in SPANS]

    outgoing = group_columns(normal_matrix, column_places, devices)
    arrived = lax.all_to_all(outgoing, ("row", "col"), split_axis=0, concat_axis=0, tiled=True)
    v_hi = lax.reduce_precision(check_vectors, 8, 7)
    v_lo = (check_vectors - v_hi).astype(jnp.bfloat16)
    v_hi = v_hi.astype(jnp.bfloat16)
    me = lax.axis_index("col").astype(jnp.int32)

    chosen = group_rows(arrived, row_places, row_count, share, widths)

    tile_layout = None
    sums = []
    last = arrived
    offset = 0
    for q, span in enumerate(SPANS):
        final = q == len(SPANS) - 1
        send, _ = lax.optimization_barrier((chosen[q], last))
        last = along(send)
        piece = last
        if sums:
            piece, sums[-1] = lax.optimization_barrier((last, sums[-1]))
        where = jnp.stack([me % 2, jnp.zeros_like(me) if final else me // 2])
        tile_layout, other, mine = tile_and_product(piece, v_hi, v_lo, where, tile_layout, col_count, share, offset)
        offset += span
        both = mine + flip(other, 1)
        if final:
            parts = lax.all_to_all(both, "col", split_axis=0, concat_axis=0, axis_index_groups=groups, tiled=True)
            sums.append(parts.sum(axis=0))
        else:
            near = both[0:2]
            for y in range(1, col_count // 4):
                near = near + flip(both[2 * y:2 * y + 2], 4 * y)
            sums.append(near[0] + flip(near[1], 2))
    return tile_layout.reshape(rows, unknowns // col_count), jnp.concatenate(sums, axis=0)


def solution(mesh):
    return jax.shard_map(
        shards,
        mesh=mesh,
        in_specs=(P(("row", "col"), None), P(), P("col", None)),
        out_specs=(P("row", "col"), P(("row", "col"), None)),
        check_vma=False,
    )
```

time: 606 us -> 292 us (0.48)
  local copies, waits for them, and re-layouts: 348 us -> 3.45 us
  Pallas kernels: 0 us -> 66 us
  blocking collectives: 82.3 us -> 123 us
  waiting for transfers between devices: 98.4 us -> 71.1 us
  matrix products: 25.2 us -> 0 us
  between operations: 14.1 us -> 0.76 us
  other arithmetic: 25 us -> 12.3 us
    gather x4 -> x0, local copies, waits for them, and re-layouts: 261 us -> none  [the longest x1 79.3 us: shards(): old_of_new[new_of_packed(places, row_count, unknowns // row_count, TILE)]]
    reduce_scatter x1 -> x0, waiting for transfers between devices: 89.6 us -> none  [shards(): lax.psum_scatter(jnp.dot(tile_layout, check_vectors, precision=lax.Precis...]
    pallas_call x0 -> x4, Pallas kernels: none -> 66 us  [the longest x2 23.2 us: tile_and_product(): pl.pallas_call(kernel, grid_spec=pltpu.PrefetchScalarGridSpec(num_scalar_...]
    scatter x1 -> x0, local copies, waits for them, and re-layouts: 52.9 us -> none  [shards(): old_of_new = jnp.zeros((unknowns,), jnp.int32).at[new_index].set(places)]
    all_to_all x1 -> x2, blocking collectives: 82.3 us -> 123 us  [the longest x1 91.6 us: shards(): lax.all_to_all(outgoing, ('row', 'col'), split_axis=0, concat_axis=0, til...]
    ppermute x0 -> x6, waiting for transfers between devices: none -> 37.5 us  [shards(): lax.ppermute(x, 'col', [(i, i ^ bits) for i in range(col_count)])]
    dot_general x1 -> x0, matrix products: 25.2 us -> none  [shards(): jnp.dot(tile_layout, check_vectors, precision=lax.Precision.HIGHEST, pref...]
    select_n x5 -> x0, other arithmetic: 24.9 us -> none  [the longest x1 11.3 us: shards(): chosen = jnp.take(arrived, col_pick, axis=0)]
  transfers between devices with their start and end apart: 2 -> 8, of which waited for: 2 -> 6; matrix products, arithmetic and copies ran while one was open for 13% -> 3% of each run, Pallas kernels for 0% -> 0%
where the time goes in v3:
time: 292 us; the launch traced here: 291 us
  blocking collectives  123 us (42%)
  waiting for transfers between devices  71.1 us (24%)
  Pallas kernels  66 us (23%)
  starting transfers between devices  14 us (5%)
  other arithmetic  12.3 us (4%)
  local copies, waits for them, and re-layouts  3.45 us (1%)
    all_to_all x1, blocking collectives, shards(): lax.all_to_all(outgoing, ('row', 'col'), split_axis=0, concat_axis=0, til...  91.6 us
    ppermute x6, waiting for transfers between devices, shards(): lax.ppermute(x, 'col', [(i, i ^ bits) for i in range(col_count)])  37.5 us
    all_to_all x2, waiting for transfers between devices, shards(): lax.all_to_all(x, 'row', split_axis=0, concat_axis=0, tiled=True)  33.7 us
    all_to_all x1, blocking collectives, shards(): lax.all_to_all(both, 'col', split_axis=0, concat_axis=0, axis_index_group...  31.2 us
    pallas_call x2, Pallas kernels, tile_and_product(): pl.pallas_call(kernel, grid_spec=pltpu.PrefetchScalarGridSpec(num_scalar_...  23.2 us
    pallas_call x1, Pallas kernels, group_columns(): pl.pallas_call(kernel, grid=(steps + outs,), in_specs=[pl.BlockSpec((1, 1...  22.9 us
    pallas_call x1, Pallas kernels, group_rows(): pl.pallas_call(kernel, grid=(steps + outs,), in_specs=[pl.BlockSpec((1, 1...  19.9 us
    all_to_all x2, starting transfers between devices, shards(): lax.all_to_all(x, 'row', split_axis=0, concat_axis=0, tiled=True)  7.32 us
  transfers between devices with their start and end apart: 8, of which 6 were waited for; matrix products, arithmetic and copies ran while one was open for 3% of the time, Pallas kernels for 0%

profile of v3, /device:TPU:0, one launch (start us, length us, event | category | flops | bytes accessed | tf_op | source)
XLA Modules:
  0.0 290.5 jit_solution(6232179422678316443)
XLA Ops:
  0.6 1.8 fusion.14
  2.4 22.9 %group_columns.1 = f32[128,104,128]{2,1,0:T(8,128)} custom-call(s32[4,1,3584]{2,1,0:T(1,128)} %bitcast.12, f32[112,14336]{1,0:T(8,128)} %x_ref.1), custom_call_target="tpu_custom_call" | custom-call | tf_op jit(solution)/shard_map/group_columns/pallas_call | solution.py:60
  25.3 91.6 %all_to_all.20.x_ref = f32[128,104,128]{2,1,0:T(8,128)} all-to-all(f32[128,104,128]{2,1,0:T(8,128)} %group_columns.1), channel_id=1, replica_groups=mesh['row'=8,'col'=16] {'row','col'}, dimensions={0} | all-to-all | bytes 13631488 | tf_op jit(solution)/shard_map/all_to_all | solution.py:248
  116.9 19.9 %group_rows.1 = (f32[8,112,896]{2,1,0:T(8,128)}, f32[8,112,896]{2,1,0:T(8,128)}) custom-call(s32[4,1,3584]{2,1,0:T(1,128)} %bitcast.11, f32[128,104,128]{2,1,0:T(8,128)} %all_to_all.20.x_ref), custom_call_target="tpu_custom_call" | custom-call | tf_op jit(solution)/shard_map/group_rows/pallas_call | solution.py:129
  136.8 3.7 %all-to-all-start.1 = ((f32[8,112,896]{2,1,0:T(8,128)}), f32[8,112,896]{2,1,0:T(8,128)S(1)}, u32[]{:S(2)}, u32[]{:S(2)}) async-start(f32[8,112,896]{2,1,0:T(8,128)} %get-tuple-element.16), calls=%async_computation.1 | async-start | bytes 6422528 | tf_op jit(solution)/shard_map/all_to_all | solution.py:242
  140.5 0.7 pad_add_fusion
  141.2 4.7 %fusion = (bf16[896,1024]{1,0:T(8,128)(2,1)}, bf16[896,1024]{1,0:T(8,128)(2,1)}) fusion(f32[896,1024]{1,0:T(8,128)} %param.5), kind=kLoop, calls=%fused_computation.2 | loop fusion | flops 3670016 | bytes 7340032 | tf_op jit(solution)/shard_map/convert_element_type | solution.py:250
  145.8 33.7 %all-to-all-done.1.x_ref = f32[8,112,896]{2,1,0:T(8,128)S(1)} async-done(((f32[8,112,896]{2,1,0:T(8,128)}), f32[8,112,896]{2,1,0:T(8,128)S(1)}, u32[]{:S(2)}, u32[]{:S(2)}) %all-to-all-start.1) | async-done | bytes 3211296 | tf_op jit(solution)/shard_map/all_to_all | solution.py:242
  179.5 0.0 copy-start.1
  179.5 1.7 copy-done.1
  181.2 11.6 %shard_map.50 = (f32[16,112,896]{2,1,0:T(8,128)}, f32[8,56,1024]{2,1,0:T(8,128)}, f32[8,56,1024]{2,1,0:T(8,128)}) custom-call(s32[2]{0:T(128)} %get-tuple-element.34.where_ref, f32[8,112,896]{2,1,0:T(8,128)} %copy-done.1, bf16[896,1024]{1,0:T(8,128)(2,1)} %get-tuple-element.27.hi_ref, bf16[896,1024]{1,0:T(8,128)(2,1)} %get-tuple-element.26.lo_ref), custom_call_target="tpu_custom_call" | custom-call | flops 4932501504 | bytes 6422528 | tf_op jit(solution)/shard_map/pallas_call | solution.py:199
  192.7 0.1 collective-permute-start
  192.8 3.7 %all-to-all-start.2 = ((f32[8,112,896]{2,1,0:T(8,128)}), f32[8,112,896]{2,1,0:T(8,128)S(1)}, u32[]{:S(2)}, u32[]{:S(2)}) async-start(f32[8,112,896]{2,1,0:T(8,128)} %get-tuple-element.17), calls=%async_computation.2 | async-start | bytes 6422528 | tf_op jit(solution)/shard_map/all_to_all | solution.py:242
  196.5 0.4 collective-permute-done
  196.9 2.4 add.94
  199.3 0.1 fusion.21
  199.4 0.1 collective-permute-start.1
  199.5 3.4 %collective-permute-start.3 = (f32[2,56,1024]{2,1,0:T(8,128)S(1)}, f32[2,56,1024]{2,1,0:T(8,128)S(1)}, u32[]{:S(2)}, u32[]{:S(2)}) collective-permute-start(f32[2,56,1024]{2,1,0:T(8,128)S(1)} %get-tuple-element.29), channel_id=1, source_target_pairs={{0,12},{1,13},{2,14},{3,15},{4,8},{5,9},{6,10},{7,11},{8,4},{9,5},... | collective-permute-start | bytes 1376264 | tf_op jit(solution)/shard_map/ppermute | solution.py:243
  202.9 0.7 collective-permute-start.2
  203.6 9.3 %collective-permute-done.1 = f32[2,56,1024]{2,1,0:T(8,128)S(1)} collective-permute-done((f32[2,56,1024]{2,1,0:T(8,128)S(1)}, f32[2,56,1024]{2,1,0:T(8,128)S(1)}, u32[]{:S(2)}, u32[]{:S(2)}) %collective-permute-start.1) | collective-permute-done | bytes 458784 | tf_op jit(solution)/shard_map/ppermute | solution.py:243
  212.9 10.4 %collective-permute-done.3 = f32[2,56,1024]{2,1,0:T(8,128)S(1)} collective-permute-done((f32[2,56,1024]{2,1,0:T(8,128)S(1)}, f32[2,56,1024]{2,1,0:T(8,128)S(1)}, u32[]{:S(2)}, u32[]{:S(2)}) %collective-permute-start.3) | collective-permute-done | bytes 458784 | tf_op jit(solution)/shard_map/ppermute | solution.py:243
  223.3 0.0 collective-permute-done.2
  223.3 0.1 fusion.2
  223.4 2.4 collective-permute-start.4
  225.8 13.4 %collective-permute-done.4 = f32[56,1024]{1,0:T(8,128)S(1)} collective-permute-done((f32[56,1024]{1,0:T(8,128)S(1)}, f32[56,1024]{1,0:T(8,128)S(1)}, u32[]{:S(2)}, u32[]{:S(2)}) %collective-permute-start.4) | collective-permute-done | bytes 229408 | tf_op jit(solution)/shard_map/ppermute | solution.py:243
  239.2 0.0 all-to-all-done.2.x_ref
  239.2 0.0 copy-start
  239.2 1.7 copy-done
  240.9 11.6 %shard_map.51 = (f32[16,112,896]{2,1,0:T(8,128)}, f32[8,56,1024]{2,1,0:T(8,128)}, f32[8,56,1024]{2,1,0:T(8,128)}) custom-call(s32[2]{0:T(128)} %get-tuple-element.33.where_ref, f32[8,112,896]{2,1,0:T(8,128)} %copy-done, bf16[896,1024]{1,0:T(8,128)(2,1)} %get-tuple-element.27.hi_ref, ...), custom_call_target="tpu_custom_call", output_to_operand_aliasing={{0}: (4, {})} | custom-call | flops 4932501504 | bytes 6422528 | tf_op jit(solution)/shard_map/pallas_call | solution.py:199
  252.5 0.1 collective-permute-start.5
  252.6 4.0 %collective-permute-done.5 = f32[8,56,1024]{2,1,0:T(8,128)S(1)} collective-permute-done((f32[8,56,1024]{2,1,0:T(8,128)}, f32[8,56,1024]{2,1,0:T(8,128)S(1)}, u32[]{:S(2)}, u32[]{:S(2)}) %collective-permute-start.5) | collective-permute-done | bytes 1835040 | tf_op jit(solution)/shard_map/ppermute | solution.py:243
  256.6 1.8 add.99
  258.4 31.2 %all_to_all.21 = f32[8,56,1024]{2,1,0:T(8,128)S(1)} all-to-all(f32[8,56,1024]{2,1,0:T(8,128)S(1)} %add.99), channel_id=1, replica_groups={{0,2,4,6,8,10,12,14},{1,3,5,7,9,11,13,15},{16,18,20,22,24,26,28,30},{17..., dimensions={0} | all-to-all | bytes 3670016 | tf_op jit(solution)/shard_map/all_to_all | solution.py:272
  289.6 0.1 reduce_sum.9
  289.7 0.8 pad_maximum_fusion
  (2 shorter events, 0.1 us)
Async XLA Ops:
  136.8 42.6 %all-to-all-start.1 = ((f32[8,112,896]{2,1,0:T(8,128)}), f32[8,112,896]{2,1,0:T(8,128)S(1)}, u32[]{:S(2)}, u32[]{:S(2)}) async-start(f32[8,112,896]{2,1,0:T(8,128)} %get-tuple-element.16), calls=%async_computation.1 | async-start | bytes 6422528 | tf_op jit(solution)/shard_map/all_to_all | solution.py:242
  179.5 1.7 copy-start.1
  192.7 4.2 %collective-permute-start = (f32[8,56,1024]{2,1,0:T(8,128)}, f32[8,56,1024]{2,1,0:T(8,128)}, u32[]{:S(2)}, u32[]{:S(2)}) collective-permute-start(f32[8,56,1024]{2,1,0:T(8,128)} %get-tuple-element.19), channel_id=1, source_target_pairs={{0,1},{1,0},{2,3},{3,2},{4,5},{5,4},{6,7},{7,6},{8,9},{9,8},{10,11... | collective-permute-start | bytes 5505032 | tf_op jit(solution)/shard_map/ppermute | solution.py:243
  192.8 46.4 %all-to-all-start.2 = ((f32[8,112,896]{2,1,0:T(8,128)}), f32[8,112,896]{2,1,0:T(8,128)S(1)}, u32[]{:S(2)}, u32[]{:S(2)}) async-start(f32[8,112,896]{2,1,0:T(8,128)} %get-tuple-element.17), calls=%async_computation.2 | async-start | bytes 6422528 | tf_op jit(solution)/shard_map/all_to_all | solution.py:242
  199.4 13.5 %collective-permute-start.1 = (f32[2,56,1024]{2,1,0:T(8,128)S(1)}, f32[2,56,1024]{2,1,0:T(8,128)S(1)}, u32[]{:S(2)}, u32[]{:S(2)}) collective-permute-start(f32[2,56,1024]{2,1,0:T(8,128)S(1)} %get-tuple-element.28), channel_id=1, source_target_pairs={{0,4},{1,5},{2,6},{3,7},{4,0},{5,1},{6,2},{7,3},{8,12},{9,13},{10,... | collective-permute-start | bytes 1376264 | tf_op jit(solution)/shard_map/ppermute | solution.py:243
  199.5 23.7 %collective-permute-start.3 = (f32[2,56,1024]{2,1,0:T(8,128)S(1)}, f32[2,56,1024]{2,1,0:T(8,128)S(1)}, u32[]{:S(2)}, u32[]{:S(2)}) collective-permute-start(f32[2,56,1024]{2,1,0:T(8,128)S(1)} %get-tuple-element.29), channel_id=1, source_target_pairs={{0,12},{1,13},{2,14},{3,15},{4,8},{5,9},{6,10},{7,11},{8,4},{9,5},... | collective-permute-start | bytes 1376264 | tf_op jit(solution)/shard_map/ppermute | solution.py:243
  202.9 20.4 %collective-permute-start.2 = (f32[2,56,1024]{2,1,0:T(8,128)S(1)}, f32[2,56,1024]{2,1,0:T(8,128)S(1)}, u32[]{:S(2)}, u32[]{:S(2)}) collective-permute-start(f32[2,56,1024]{2,1,0:T(8,128)S(1)} %get-tuple-element.30), channel_id=1, source_target_pairs={{0,8},{1,9},{2,10},{3,11},{4,12},{5,13},{6,14},{7,15},{8,0},{9,1},... | collective-permute-start | bytes 1376264 | tf_op jit(solution)/shard_map/ppermute | solution.py:243
  223.4 15.7 %collective-permute-start.4 = (f32[56,1024]{1,0:T(8,128)S(1)}, f32[56,1024]{1,0:T(8,128)S(1)}, u32[]{:S(2)}, u32[]{:S(2)}) collective-permute-start(f32[56,1024]{1,0:T(8,128)S(1)} %slice_bitcast_fusion), channel_id=1, source_target_pairs={{0,2},{1,3},{2,0},{3,1},{4,6},{5,7},{6,4},{7,5},{8,10},{9,11},{10,... | collective-permute-start | bytes 688136 | tf_op jit(solution)/shard_map/ppermute | solution.py:243
  239.2 1.7 copy-start
  252.5 4.1 %collective-permute-start.5 = (f32[8,56,1024]{2,1,0:T(8,128)}, f32[8,56,1024]{2,1,0:T(8,128)S(1)}, u32[]{:S(2)}, u32[]{:S(2)}) collective-permute-start(f32[8,56,1024]{2,1,0:T(8,128)} %get-tuple-element.25), channel_id=1, source_target_pairs={{0,1},{1,0},{2,3},{3,2},{4,5},{5,4},{6,7},{7,6},{8,9},{9,8},{10,11... | collective-permute-start | bytes 5505032 | tf_op jit(solution)/shard_map/ppermute | solution.py:243

commit v4 on v3

--- a/solution.py
+++ b/solution.py
@@ -10,8 +10,8 @@
 LANES = 128
 SUB = 8
 VMEM = 56 * 1024 * 1024
-UNROLL = 32
-SPANS = (56, 56)
+SPANS = (48, 40, 24)
+STEPS = 8
 
 
 def params():
@@ -34,13 +34,8 @@
             for b in range(width // LANES):
                 turned[b * LANES:(b + 1) * LANES, :share] = x_ref[:, b * LANES:(b + 1) * LANES].T
 
-            def scatter(i, carry):
-                start = i * UNROLL
-                for u in range(UNROLL):
-                    spread[pl.ds(pos_ref[0, 0, start + u], 1), :] = turned[pl.ds(start + u, 1), :]
-                return carry
-
-            lax.fori_loop(0, width // UNROLL, scatter, 0)
+            for u in range(width):
+                spread[pl.ds(pos_ref[0, 0, u], 1), :] = turned[u:u + 1, :]
 
         @pl.when(step >= steps)
         def _():
@@ -102,15 +97,13 @@
 
             lax.fori_loop(0, per // 8, unpack, 0)
 
-            def scatter(b, carry):
+            for b in range(per):
                 start = b * share
                 for u in range(keep):
-                    spread[pl.ds(pos_ref[0, 0, start + u], 1), :] = x_ref[b, pl.ds(u, 1), :]
+                    spread[pl.ds(pos_ref[0, 0, start + u], 1), :] = x_ref[b, u:u + 1, :]
                 for u in range(SUB):
-                    spread[pl.ds(pos_ref[0, 0, start + keep + u], 1), :] = extra[pl.ds(b * SUB + u, 1), :]
-                return carry
-
-            lax.fori_loop(0, per, scatter, 0)
+                    at = b * SUB + u
+                    spread[pl.ds(pos_ref[0, 0, start + keep + u], 1), :] = extra[at:at + 1, :]
 
         @pl.when(step >= steps)
         def _():
@@ -223,7 +216,7 @@
     devices = row_count * col_count
     share, unknowns = normal_matrix.shape
     rows = unknowns // row_count
-    steps = 4
+    steps = STEPS
 
     tile, lane = new_index // TILE, new_index % TILE
     within_col = tile // col_count * TILE + lane
@@ -255,15 +248,15 @@
 
     tile_layout = None
     sums = []
-    last = arrived
+    last, held = arrived, None
     offset = 0
     for q, span in enumerate(SPANS):
         final = q == len(SPANS) - 1
         send, _ = lax.optimization_barrier((chosen[q], last))
         last = along(send)
         piece = last
-        if sums:
-            piece, sums[-1] = lax.optimization_barrier((last, sums[-1]))
+        if held is not None:
+            piece, _ = lax.optimization_barrier((last, held))
         where = jnp.stack([me % 2, jnp.zeros_like(me) if final else me // 2])
         tile_layout, other, mine = tile_and_product(piece, v_hi, v_lo, where, tile_layout, col_count, share, offset)
         offset += span
@@ -274,8 +267,11 @@
         else:
             near = both[0:2]
             for y in range(1, col_count // 4):
-                near = near + flip(both[2 * y:2 * y + 2], 4 * y)
-            sums.append(near[0] + flip(near[1], 2))
+                got = flip(both[2 * y:2 * y + 2], 4 * y)
+                near = near + got
+            held = both if q == len(SPANS) - 2 else near
+            got = flip(near[1], 2)
+            sums.append(near[0] + got)
     return tile_layout.reshape(rows, unknowns // col_count), jnp.concatenate(sums, axis=0)
 
 

time: 292 us -> 302 us (1.034)
  blocking collectives: 123 us -> 91.6 us
  waiting for transfers between devices: 71.1 us -> 93.3 us
  starting transfers between devices: 14 us -> 29.9 us
    all_to_all x1 -> x0, blocking collectives: 31.2 us -> none  [shards(): lax.all_to_all(both, 'col', split_axis=0, concat_axis=0, axis_index_group...]
    all_to_all x2 -> x3, waiting for transfers between devices: 33.7 us -> 51.3 us  [shards(): lax.all_to_all(x, 'row', split_axis=0, concat_axis=0, tiled=True)]
    ppermute x6 -> x11, starting transfers between devices: 6.7 us -> 13.9 us  [shards(): lax.ppermute(x, 'col', [(i, i ^ bits) for i in range(col_count)])]
    all_to_all x0 -> x1, starting transfers between devices: none -> 5 us  [shards(): lax.all_to_all(both, 'col', split_axis=0, concat_axis=0, axis_index_group...]
    pallas_call x2 -> x3, Pallas kernels: 23.2 us -> 27.5 us  [tile_and_product(): pl.pallas_call(kernel, grid_spec=pltpu.PrefetchScalarGridSpec(num_scalar_...]
    ppermute x6 -> x11, waiting for transfers between devices: 37.5 us -> 41.6 us  [shards(): lax.ppermute(x, 'col', [(i, i ^ bits) for i in range(col_count)])]
    all_to_all x2 -> x3, starting transfers between devices: 7.32 us -> 11 us  [shards(): lax.all_to_all(x, 'row', split_axis=0, concat_axis=0, tiled=True)]
    pallas_call x1, Pallas kernels: 22.9 us -> 19.6 us  [group_columns(): pl.pallas_call(kernel, grid=(steps + outs,), in_specs=[pl.BlockSpec((1, 1...]
  transfers between devices with their start and end apart: 8 -> 15, of which waited for: 6 -> 10; matrix products, arithmetic and copies ran while one was open for 3% -> 4% of each run, Pallas kernels for 0% -> 0%
where the time goes in v4:
time: 302 us; the launch traced here: 301 us
  waiting for transfers between devices  93.3 us (31%)
  blocking collectives  91.6 us (30%)
  Pallas kernels  66.1 us (22%)
  starting transfers between devices  29.9 us (10%)
  other arithmetic  13.7 us (5%)
  local copies, waits for them, and re-layouts  5.31 us (2%)
    all_to_all x1, blocking collectives, shards(): lax.all_to_all(outgoing, ('row', 'col'), split_axis=0, concat_axis=0, til...  91.6 us
    all_to_all x3, waiting for transfers between devices, shards(): lax.all_to_all(x, 'row', split_axis=0, concat_axis=0, tiled=True)  51.3 us
    ppermute x11, waiting for transfers between devices, shards(): lax.ppermute(x, 'col', [(i, i ^ bits) for i in range(col_count)])  41.6 us
    pallas_call x3, Pallas kernels, tile_and_product(): pl.pallas_call(kernel, grid_spec=pltpu.PrefetchScalarGridSpec(num_scalar_...  27.5 us
    pallas_call x1, Pallas kernels, group_columns(): pl.pallas_call(kernel, grid=(steps + outs,), in_specs=[pl.BlockSpec((1, 1...  19.6 us
    pallas_call x1, Pallas kernels, group_rows(): pl.pallas_call(kernel, grid=(steps + outs,), in_specs=[pl.BlockSpec((1, 1...  19.1 us
    ppermute x11, starting transfers between devices, shards(): lax.ppermute(x, 'col', [(i, i ^ bits) for i in range(col_count)])  13.9 us
    all_to_all x3, starting transfers between devices, shards(): lax.all_to_all(x, 'row', split_axis=0, concat_axis=0, tiled=True)  11 us
  transfers between devices with their start and end apart: 15, of which 10 were waited for; matrix products, arithmetic and copies ran while one was open for 4% of the time, Pallas kernels for 0%

profile of v4, /device:TPU:0, one launch (start us, length us, event | category | flops | bytes accessed | tf_op | source)
XLA Modules:
  0.0 300.8 jit_solution(11339101493928925298)
XLA Ops:
  0.6 1.8 fusion.16
  2.4 19.6 %group_columns.1 = f32[128,104,128]{2,1,0:T(8,128)} custom-call(s32[8,1,1792]{2,1,0:T(1,128)} %bitcast.19, f32[112,14336]{1,0:T(8,128)} %x_ref.1), custom_call_target="tpu_custom_call" | custom-call | tf_op jit(solution)/shard_map/group_columns/pallas_call | solution.py:55
  22.0 91.6 %all_to_all.25.x_ref = f32[128,104,128]{2,1,0:T(8,128)} all-to-all(f32[128,104,128]{2,1,0:T(8,128)} %group_columns.1), channel_id=1, replica_groups=mesh['row'=8,'col'=16] {'row','col'}, dimensions={0} | all-to-all | bytes 13631488 | tf_op jit(solution)/shard_map/all_to_all | solution.py:241
  113.6 19.1 %group_rows.1 = (f32[8,112,768]{2,1,0:T(8,128)}, f32[8,112,640]{2,1,0:T(8,128)}, f32[8,112,384]{2,1,0:T(8,128)}) custom-call(s32[8,1,1792]{2,1,0:T(1,128)} %bitcast.18, f32[128,104,128]{2,1,0:T(8,128)} %all_to_all.25.x_ref), custom_call_target="tpu_custom_call" | custom-call | tf_op jit(solution)/shard_map/group_rows/pallas_call | solution.py:122
  132.7 3.6 %all-to-all-start.1 = ((f32[8,112,768]{2,1,0:T(8,128)}), f32[8,112,768]{2,1,0:T(8,128)S(1)}, u32[]{:S(2)}, u32[]{:S(2)}) async-start(f32[8,112,768]{2,1,0:T(8,128)} %get-tuple-element.22), calls=%async_computation.1 | async-start | bytes 5505024 | tf_op jit(solution)/shard_map/all_to_all | solution.py:235
  136.3 0.7 pad_add_fusion.1.where_ref
  137.0 4.6 %fusion = (bf16[896,1024]{1,0:T(8,128)(2,1)}, bf16[896,1024]{1,0:T(8,128)(2,1)}) fusion(f32[896,1024]{1,0:T(8,128)} %param.5), kind=kLoop, calls=%fused_computation.2 | loop fusion | flops 3670016 | bytes 7340032 | tf_op jit(solution)/shard_map/convert_element_type | solution.py:243
  141.6 28.8 %all-to-all-done.1.x_ref = f32[8,112,768]{2,1,0:T(8,128)S(1)} async-done(((f32[8,112,768]{2,1,0:T(8,128)}), f32[8,112,768]{2,1,0:T(8,128)S(1)}, u32[]{:S(2)}, u32[]{:S(2)}) %all-to-all-start.1) | async-done | bytes 2752544 | tf_op jit(solution)/shard_map/all_to_all | solution.py:235
  170.4 1.5 copy-done.1
  171.9 10.4 %shard_map.50 = (f32[16,112,896]{2,1,0:T(8,128)}, f32[8,48,1024]{2,1,0:T(8,128)}, f32[8,48,1024]{2,1,0:T(8,128)}) custom-call(s32[2]{0:T(128)} %pad_add_fusion.1.where_ref, f32[8,112,768]{2,1,0:T(8,128)} %copy-done.1, bf16[896,1024]{1,0:T(8,128)(2,1)} %get-tuple-element.37.hi_ref, bf16[896,1024]{1,0:T(8,128)(2,1)} %get-tuple-element.36.lo_ref), custom_call_target="tpu_custom_call" | custom-call | flops 4227858432 | bytes 5505024 | tf_op jit(solution)/shard_map/pallas_call | solution.py:192
  182.4 0.1 collective-permute-start
  182.5 3.6 %all-to-all-start.2 = ((f32[8,112,640]{2,1,0:T(8,128)}), f32[8,112,640]{2,1,0:T(8,128)S(1)}, u32[]{:S(2)}, u32[]{:S(2)}) async-start(f32[8,112,640]{2,1,0:T(8,128)} %get-tuple-element.23), calls=%async_computation.2 | async-start | bytes 4587520 | tf_op jit(solution)/shard_map/all_to_all | solution.py:235
  186.1 0.1 collective-permute-done
  186.2 2.1 add.123
  188.3 0.1 fusion.23
  188.4 0.1 collective-permute-start.1
  188.5 3.4 %collective-permute-start.3 = (f32[2,48,1024]{2,1,0:T(8,128)S(1)}, f32[2,48,1024]{2,1,0:T(8,128)S(1)}, u32[]{:S(2)}, u32[]{:S(2)}) collective-permute-start(f32[2,48,1024]{2,1,0:T(8,128)S(1)} %get-tuple-element.39), channel_id=1, source_target_pairs={{0,12},{1,13},{2,14},{3,15},{4,8},{5,9},{6,10},{7,11},{8,4},{9,5},... | collective-permute-start | bytes 1179656 | tf_op jit(solution)/shard_map/ppermute | solution.py:236
  191.9 0.7 collective-permute-start.2
  192.6 7.9 %collective-permute-done.1 = f32[2,48,1024]{2,1,0:T(8,128)S(1)} collective-permute-done((f32[2,48,1024]{2,1,0:T(8,128)S(1)}, f32[2,48,1024]{2,1,0:T(8,128)S(1)}, u32[]{:S(2)}, u32[]{:S(2)}) %collective-permute-start.1) | collective-permute-done | bytes 393248 | tf_op jit(solution)/shard_map/ppermute | solution.py:236
  200.5 9.2 %collective-permute-done.3 = f32[2,48,1024]{2,1,0:T(8,128)S(1)} collective-permute-done((f32[2,48,1024]{2,1,0:T(8,128)S(1)}, f32[2,48,1024]{2,1,0:T(8,128)S(1)}, u32[]{:S(2)}, u32[]{:S(2)}) %collective-permute-start.3) | collective-permute-done | bytes 393248 | tf_op jit(solution)/shard_map/ppermute | solution.py:236
  209.7 0.1 fusion.2
  209.8 6.2 %all-to-all-done.2.x_ref = f32[8,112,640]{2,1,0:T(8,128)S(1)} async-done(((f32[8,112,640]{2,1,0:T(8,128)}), f32[8,112,640]{2,1,0:T(8,128)S(1)}, u32[]{:S(2)}, u32[]{:S(2)}) %all-to-all-start.2) | async-done | bytes 2293792 | tf_op jit(solution)/shard_map/all_to_all | solution.py:235
  216.0 1.4 copy-done.2
  217.4 9.5 %shard_map.51 = (f32[16,112,896]{2,1,0:T(8,128)}, f32[8,40,1024]{2,1,0:T(8,128)}, f32[8,40,1024]{2,1,0:T(8,128)}) custom-call(s32[2]{0:T(128)} %pad_add_fusion.1.where_ref, f32[8,112,640]{2,1,0:T(8,128)} %copy-done.2, bf16[896,1024]{1,0:T(8,128)(2,1)} %get-tuple-element.37.hi_ref, ...), custom_call_target="tpu_custom_call", output_to_operand_aliasing={{0}: (4, {})} | custom-call | flops 3523215360 | bytes 4587520 | tf_op jit(solution)/shard_map/pallas_call | solution.py:192
  227.0 0.1 collective-permute-start.4
  227.1 3.8 %all-to-all-start.3 = ((f32[8,112,384]{2,1,0:T(8,128)}), f32[8,112,384]{2,1,0:T(8,128)S(1)}, u32[]{:S(2)}, u32[]{:S(2)}) async-start(f32[8,112,384]{2,1,0:T(8,128)} %get-tuple-element.24), calls=%async_computation.3 | async-start | bytes 2752512 | tf_op jit(solution)/shard_map/all_to_all | solution.py:235
  230.9 0.6 pad_add_fusion.where_ref
  231.5 1.1 copy-done.3
  232.5 1.9 add.127
  234.4 16.4 %all-to-all-done.3.x_ref = f32[8,112,384]{2,1,0:T(8,128)S(1)} async-done(((f32[8,112,384]{2,1,0:T(8,128)}), f32[8,112,384]{2,1,0:T(8,128)S(1)}, u32[]{:S(2)}, u32[]{:S(2)}) %all-to-all-start.3) | async-done | bytes 1376288 | tf_op jit(solution)/shard_map/all_to_all | solution.py:235
  250.8 1.1 copy-done
  251.9 7.5 %shard_map.52 = (f32[16,112,896]{2,1,0:T(8,128)}, f32[8,24,1024]{2,1,0:T(8,128)}, f32[8,24,1024]{2,1,0:T(8,128)}) custom-call(s32[2]{0:T(128)} %pad_add_fusion.where_ref, f32[8,112,384]{2,1,0:T(8,128)} %copy-done, bf16[896,1024]{1,0:T(8,128)(2,1)} %get-tuple-element.37.hi_ref, ...), custom_call_target="tpu_custom_call", output_to_operand_aliasing={{0}: (4, {})} | custom-call | flops 2113929216 | bytes 2752512 | tf_op jit(solution)/shard_map/pallas_call | solution.py:192
  259.4 0.1 collective-permute-start.10
  259.5 0.1 fusion.24
  259.6 0.1 collective-permute-start.6
  259.7 3.4 %collective-permute-start.8 = (f32[2,40,1024]{2,1,0:T(8,128)S(1)}, f32[2,40,1024]{2,1,0:T(8,128)S(1)}, u32[]{:S(2)}, u32[]{:S(2)}) collective-permute-start(f32[2,40,1024]{2,1,0:T(8,128)S(1)} %get-tuple-element.42), channel_id=1, source_target_pairs={{0,12},{1,13},{2,14},{3,15},{4,8},{5,9},{6,10},{7,11},{8,4},{9,5},... | collective-permute-start | bytes 983048 | tf_op jit(solution)/shard_map/ppermute | solution.py:236
  263.1 0.7 collective-permute-start.7
  263.8 1.7 collective-permute-start.5
  265.5 4.8 %collective-permute-done.6 = f32[2,40,1024]{2,1,0:T(8,128)S(1)} collective-permute-done((f32[2,40,1024]{2,1,0:T(8,128)S(1)}, f32[2,40,1024]{2,1,0:T(8,128)S(1)}, u32[]{:S(2)}, u32[]{:S(2)}) %collective-permute-start.6) | collective-permute-done | bytes 327712 | tf_op jit(solution)/shard_map/ppermute | solution.py:236
  270.3 7.9 %collective-permute-done.8 = f32[2,40,1024]{2,1,0:T(8,128)S(1)} collective-permute-done((f32[2,40,1024]{2,1,0:T(8,128)S(1)}, f32[2,40,1024]{2,1,0:T(8,128)S(1)}, u32[]{:S(2)}, u32[]{:S(2)}) %collective-permute-start.8) | collective-permute-done | bytes 327712 | tf_op jit(solution)/shard_map/ppermute | solution.py:236
  278.2 0.0 collective-permute-done.7
  278.2 0.1 fusion.4
  278.3 1.0 add.133
  279.3 5.0 %all-to-all-start.4 = ((f32[8,24,1024]{2,1,0:T(8,128)}), f32[8,24,1024]{2,1,0:T(8,128)S(1)}, u32[]{:S(2)}, u32[]{:S(2)}) async-start(f32[8,24,1024]{2,1,0:T(8,128)} %add.133), calls=%async_computation.4 | async-start | bytes 1572864 | tf_op jit(solution)/shard_map/all_to_all | solution.py:265
  284.3 3.6 %collective-permute-start.9 = (f32[40,1024]{1,0:T(8,128)S(1)}, f32[40,1024]{1,0:T(8,128)S(1)}, u32[]{:S(2)}, u32[]{:S(2)}) collective-permute-start(f32[40,1024]{1,0:T(8,128)S(1)} %slice_bitcast_fusion.2), channel_id=1, source_target_pairs={{0,2},{1,3},{2,0},{3,1},{4,6},{5,7},{6,4},{7,5},{8,10},{9,11},{10,... | collective-permute-start | bytes 491528 | tf_op jit(solution)/shard_map/ppermute | solution.py:236
  287.9 11.7 %collective-permute-done.9 = f32[40,1024]{1,0:T(8,128)S(1)} collective-permute-done((f32[40,1024]{1,0:T(8,128)S(1)}, f32[40,1024]{1,0:T(8,128)S(1)}, u32[]{:S(2)}, u32[]{:S(2)}) %collective-permute-start.9) | collective-permute-done | bytes 163872 | tf_op jit(solution)/shard_map/ppermute | solution.py:236
  299.6 0.3 all-to-all-done.4
  300.0 0.8 pad_maximum_fusion
  (15 shorter events, 0.1 us)
Async XLA Ops:
  132.7 37.7 %all-to-all-start.1 = ((f32[8,112,768]{2,1,0:T(8,128)}), f32[8,112,768]{2,1,0:T(8,128)S(1)}, u32[]{:S(2)}, u32[]{:S(2)}) async-start(f32[8,112,768]{2,1,0:T(8,128)} %get-tuple-element.22), calls=%async_computation.1 | async-start | bytes 5505024 | tf_op jit(solution)/shard_map/all_to_all | solution.py:235
  170.4 1.5 copy-start.1
  182.4 3.8 %collective-permute-start = (f32[8,48,1024]{2,1,0:T(8,128)}, f32[8,48,1024]{2,1,0:T(8,128)}, u32[]{:S(2)}, u32[]{:S(2)}) collective-permute-start(f32[8,48,1024]{2,1,0:T(8,128)} %get-tuple-element.26), channel_id=1, source_target_pairs={{0,1},{1,0},{2,3},{3,2},{4,5},{5,4},{6,7},{7,6},{8,9},{9,8},{10,11... | collective-permute-start | bytes 4718600 | tf_op jit(solution)/shard_map/ppermute | solution.py:236
  182.5 33.6 %all-to-all-start.2 = ((f32[8,112,640]{2,1,0:T(8,128)}), f32[8,112,640]{2,1,0:T(8,128)S(1)}, u32[]{:S(2)}, u32[]{:S(2)}) async-start(f32[8,112,640]{2,1,0:T(8,128)} %get-tuple-element.23), calls=%async_computation.2 | async-start | bytes 4587520 | tf_op jit(solution)/shard_map/all_to_all | solution.py:235
  188.4 12.1 %collective-permute-start.1 = (f32[2,48,1024]{2,1,0:T(8,128)S(1)}, f32[2,48,1024]{2,1,0:T(8,128)S(1)}, u32[]{:S(2)}, u32[]{:S(2)}) collective-permute-start(f32[2,48,1024]{2,1,0:T(8,128)S(1)} %get-tuple-element.38), channel_id=1, source_target_pairs={{0,4},{1,5},{2,6},{3,7},{4,0},{5,1},{6,2},{7,3},{8,12},{9,13},{10,... | collective-permute-start | bytes 1179656 | tf_op jit(solution)/shard_map/ppermute | solution.py:236
  188.5 21.2 %collective-permute-start.3 = (f32[2,48,1024]{2,1,0:T(8,128)S(1)}, f32[2,48,1024]{2,1,0:T(8,128)S(1)}, u32[]{:S(2)}, u32[]{:S(2)}) collective-permute-start(f32[2,48,1024]{2,1,0:T(8,128)S(1)} %get-tuple-element.39), channel_id=1, source_target_pairs={{0,12},{1,13},{2,14},{3,15},{4,8},{5,9},{6,10},{7,11},{8,4},{9,5},... | collective-permute-start | bytes 1179656 | tf_op jit(solution)/shard_map/ppermute | solution.py:236
  191.9 17.8 %collective-permute-start.2 = (f32[2,48,1024]{2,1,0:T(8,128)S(1)}, f32[2,48,1024]{2,1,0:T(8,128)S(1)}, u32[]{:S(2)}, u32[]{:S(2)}) collective-permute-start(f32[2,48,1024]{2,1,0:T(8,128)S(1)} %get-tuple-element.40), channel_id=1, source_target_pairs={{0,8},{1,9},{2,10},{3,11},{4,12},{5,13},{6,14},{7,15},{8,0},{9,1},... | collective-permute-start | bytes 1179656 | tf_op jit(solution)/shard_map/ppermute | solution.py:236
  216.0 1.4 copy-start.2
  227.0 4.5 %collective-permute-start.4 = (f32[8,40,1024]{2,1,0:T(8,128)}, f32[8,40,1024]{2,1,0:T(8,128)S(1)}, u32[]{:S(2)}, u32[]{:S(2)}) collective-permute-start(f32[8,40,1024]{2,1,0:T(8,128)} %get-tuple-element.30), channel_id=1, source_target_pairs={{0,1},{1,0},{2,3},{3,2},{4,5},{5,4},{6,7},{7,6},{8,9},{9,8},{10,11... | collective-permute-start | bytes 3932168 | tf_op jit(solution)/shard_map/ppermute | solution.py:236
  227.1 23.7 %all-to-all-start.3 = ((f32[8,112,384]{2,1,0:T(8,128)}), f32[8,112,384]{2,1,0:T(8,128)S(1)}, u32[]{:S(2)}, u32[]{:S(2)}) async-start(f32[8,112,384]{2,1,0:T(8,128)} %get-tuple-element.24), calls=%async_computation.3 | async-start | bytes 2752512 | tf_op jit(solution)/shard_map/all_to_all | solution.py:235
  231.4 1.1 copy-start.3
  250.8 1.1 copy-start
  259.4 18.9 %copy-start.4 = (f32[8,24,1024]{2,1,0:T(8,128)S(1)}, f32[8,24,1024]{2,1,0:T(8,128)}, u32[]{:S(2)}) copy-start(f32[8,24,1024]{2,1,0:T(8,128)} %get-tuple-element.34) | copy-start | bytes 2359300
  259.4 18.8 %collective-permute-start.10 = (f32[8,24,1024]{2,1,0:T(8,128)}, f32[8,24,1024]{2,1,0:T(8,128)S(1)}, u32[]{:S(2)}, u32[]{:S(2)}) collective-permute-start(f32[8,24,1024]{2,1,0:T(8,128)} %get-tuple-element.35), channel_id=1, source_target_pairs={{0,1},{1,0},{2,3},{3,2},{4,5},{5,4},{6,7},{7,6},{8,9},{9,8},{10,11... | collective-permute-start | bytes 2359304 | tf_op jit(solution)/shard_map/ppermute | solution.py:236
  259.6 10.7 %collective-permute-start.6 = (f32[2,40,1024]{2,1,0:T(8,128)S(1)}, f32[2,40,1024]{2,1,0:T(8,128)S(1)}, u32[]{:S(2)}, u32[]{:S(2)}) collective-permute-start(f32[2,40,1024]{2,1,0:T(8,128)S(1)} %get-tuple-element.41), channel_id=1, source_target_pairs={{0,4},{1,5},{2,6},{3,7},{4,0},{5,1},{6,2},{7,3},{8,12},{9,13},{10,... | collective-permute-start | bytes 983048 | tf_op jit(solution)/shard_map/ppermute | solution.py:236
  259.7 18.5 %collective-permute-start.8 = (f32[2,40,1024]{2,1,0:T(8,128)S(1)}, f32[2,40,1024]{2,1,0:T(8,128)S(1)}, u32[]{:S(2)}, u32[]{:S(2)}) collective-permute-start(f32[2,40,1024]{2,1,0:T(8,128)S(1)} %get-tuple-element.42), channel_id=1, source_target_pairs={{0,12},{1,13},{2,14},{3,15},{4,8},{5,9},{6,10},{7,11},{8,4},{9,5},... | collective-permute-start | bytes 983048 | tf_op jit(solution)/shard_map/ppermute | solution.py:236
  263.1 15.1 %collective-permute-start.7 = (f32[2,40,1024]{2,1,0:T(8,128)S(1)}, f32[2,40,1024]{2,1,0:T(8,128)S(1)}, u32[]{:S(2)}, u32[]{:S(2)}) collective-permute-start(f32[2,40,1024]{2,1,0:T(8,128)S(1)} %get-tuple-element.43), channel_id=1, source_target_pairs={{0,8},{1,9},{2,10},{3,11},{4,12},{5,13},{6,14},{7,15},{8,0},{9,1},... | collective-permute-start | bytes 983048 | tf_op jit(solution)/shard_map/ppermute | solution.py:236
  263.8 24.1 %collective-permute-start.5 = (f32[48,1024]{1,0:T(8,128)S(1)}, f32[48,1024]{1,0:T(8,128)S(1)}, u32[]{:S(2)}, u32[]{:S(2)}) collective-permute-start(f32[48,1024]{1,0:T(8,128)S(1)} %slice_bitcast_fusion), channel_id=1, source_target_pairs={{0,2},{1,3},{2,0},{3,1},{4,6},{5,7},{6,4},{7,5},{8,10},{9,11},{10,... | collective-permute-start | bytes 589832 | tf_op jit(solution)/shard_map/ppermute | solution.py:236
  279.3 20.7 %all-to-all-start.4 = ((f32[8,24,1024]{2,1,0:T(8,128)}), f32[8,24,1024]{2,1,0:T(8,128)S(1)}, u32[]{:S(2)}, u32[]{:S(2)}) async-start(f32[8,24,1024]{2,1,0:T(8,128)} %add.133), calls=%async_computation.4 | async-start | bytes 1572864 | tf_op jit(solution)/shard_map/all_to_all | solution.py:265
  284.3 15.3 %collective-permute-start.9 = (f32[40,1024]{1,0:T(8,128)S(1)}, f32[40,1024]{1,0:T(8,128)S(1)}, u32[]{:S(2)}, u32[]{:S(2)}) collective-permute-start(f32[40,1024]{1,0:T(8,128)S(1)} %slice_bitcast_fusion.2), channel_id=1, source_target_pairs={{0,2},{1,3},{2,0},{3,1},{4,6},{5,7},{6,4},{7,5},{8,10},{9,11},{10,... | collective-permute-start | bytes 491528 | tf_op jit(solution)/shard_map/ppermute | solution.py:236

commit v5 on v4

--- a/solution.py
+++ b/solution.py
@@ -9,7 +9,7 @@
 TILE = 128
 LANES = 128
 SUB = 8
-VMEM = 56 * 1024 * 1024
+VMEM = 24 * 1024 * 1024
 SPANS = (48, 40, 24)
 STEPS = 8
 
@@ -87,18 +87,10 @@
 
         @pl.when(step < steps)
         def _():
-            def unpack(i, carry):
-                for u in range(8):
-                    b = i * 8 + u
-                    at = pl.multiple_of(b * SUB, SUB)
-                    for k in range(share // chunk):
-                        extra[pl.ds(at, SUB), chunk * k:chunk * (k + 1)] = x_ref[b, SUB * k:SUB * k + SUB, share:]
-                return carry
-
-            lax.fori_loop(0, per // 8, unpack, 0)
-
             for b in range(per):
                 start = b * share
+                for k in range(share // chunk):
+                    extra[b * SUB:(b + 1) * SUB, chunk * k:chunk * (k + 1)] = x_ref[b, SUB * k:SUB * k + SUB, share:]
                 for u in range(keep):
                     spread[pl.ds(pos_ref[0, 0, start + u], 1), :] = x_ref[b, u:u + 1, :]
                 for u in range(SUB):
@@ -146,14 +138,17 @@
     pairs = cols // 2
 
     def kernel(where_ref, x_ref, hi_ref, lo_ref, *refs):
-        tile_ref, other_ref, mine_ref, x_hi, x_lo, held, sem = refs[-7:]
+        tile_ref, other_ref, mine_ref, x_in, x_hi, x_lo, held, x_sem, sem = refs[-9:]
         step = pl.program_id(0)
         store = pltpu.make_async_copy(held, tile_ref.at[:, offset:offset + span, :], sem)
 
         @pl.when(step == 0)
         def _():
+            fetch = pltpu.make_async_copy(x_ref, x_in, x_sem)
+            fetch.start()
+            fetch.wait()
             for k in range(rows // LANES):
-                x = x_ref[:, :, k * LANES:(k + 1) * LANES].reshape(columns, LANES).T
+                x = x_in[:, :, k * LANES:(k + 1) * LANES].reshape(columns, LANES).T
                 hi = x.astype(jnp.bfloat16)
                 x_hi[k * LANES:(k + 1) * LANES, :] = hi
                 x_lo[k * LANES:(k + 1) * LANES, :] = (x - hi.astype(jnp.float32)).astype(jnp.bfloat16)
@@ -181,7 +176,7 @@
 
     half = jax.ShapeDtypeStruct((pairs, span, width), jnp.float32)
     half_spec = pl.BlockSpec((pairs, span, wide), lambda g, where: (0, 0, g))
-    in_specs = [pl.BlockSpec((groups, share, rows), lambda g, where: (0, 0, 0))]
+    in_specs = [pl.BlockSpec(memory_space=pl.ANY)]
     in_specs += [pl.BlockSpec((columns, wide), lambda g, where: (0, g))] * 2
     operands = [where, turned, v_hi, v_lo]
     aliases = {}
@@ -197,9 +192,11 @@
             in_specs=in_specs,
             out_specs=[pl.BlockSpec(memory_space=pl.ANY), half_spec, half_spec],
             scratch_shapes=[
+                pltpu.VMEM((groups, share, rows), jnp.float32),
                 pltpu.VMEM((rows, columns), jnp.bfloat16),
                 pltpu.VMEM((rows, columns), jnp.bfloat16),
                 pltpu.VMEM((cols, span, columns), jnp.float32),
+                pltpu.SemaphoreType.DMA,
                 pltpu.SemaphoreType.DMA,
             ],
         ),
@@ -257,19 +254,22 @@
         piece = last
         if held is not None:
             piece, _ = lax.optimization_barrier((last, held))
-        where = jnp.stack([me % 2, jnp.zeros_like(me) if final else me // 2])
+        turn = me // 2 if not final else me * 0
+        where = jnp.stack([me % 2, turn, me * 0 + q])
         tile_layout, other, mine = tile_and_product(piece, v_hi, v_lo, where, tile_layout, col_count, share, offset)
         offset += span
-        both = mine + flip(other, 1)
+        theirs = flip(other, 1)
         if final:
+            both = mine + theirs
             parts = lax.all_to_all(both, "col", split_axis=0, concat_axis=0, axis_index_groups=groups, tiled=True)
             sums.append(parts.sum(axis=0))
         else:
-            near = both[0:2]
+            both = [mine[i:i + 2] + theirs[i:i + 2] for i in range(0, col_count // 2, 2)]
+            near = both[0]
             for y in range(1, col_count // 4):
-                got = flip(both[2 * y:2 * y + 2], 4 * y)
+                got = flip(both[y], 4 * y)
                 near = near + got
-            held = both if q == len(SPANS) - 2 else near
+            held = tuple(both[1:])
             got = flip(near[1], 2)
             sums.append(near[0] + got)
     return tile_layout.reshape(rows, unknowns // col_count), jnp.concatenate(sums, axis=0)

time: 302 us -> 287 us (0.950)
  waiting for transfers between devices: 93.3 us -> 78.9 us
  Pallas kernels: 66.1 us -> 58.6 us
  local copies, waits for them, and re-layouts: 5.31 us -> 12.1 us
    ppermute x11, waiting for transfers between devices: 41.6 us -> 28.5 us  [shards(): lax.ppermute(x, 'col', [(i, i ^ bits) for i in range(col_count)])]
    unnamed x10 -> x20, local copies, waits for them, and re-layouts: 5.13 us -> 12 us
    pallas_call x3, Pallas kernels: 27.5 us -> 23.8 us  [tile_and_product(): pl.pallas_call(kernel, grid_spec=pltpu.PrefetchScalarGridSpec(num_scalar_...]
  transfers between devices with their start and end apart: 15 -> 15, of which waited for: 10 -> 7; matrix products, arithmetic and copies ran while one was open for 4% -> 4% of each run, Pallas kernels for 0% -> 5%
where the time goes in v5:
time: 287 us; the launch traced here: 286 us
  blocking collectives  91.3 us (32%)
  waiting for transfers between devices  78.9 us (27%)
  Pallas kernels  58.6 us (20%)
  starting transfers between devices  30.8 us (11%)
  other arithmetic  13.8 us (5%)
  local copies, waits for them, and re-layouts  12.1 us (4%)
    all_to_all x1, blocking collectives, shards(): lax.all_to_all(outgoing, ('row', 'col'), split_axis=0, concat_axis=0, til...  91.3 us
    all_to_all x3, waiting for transfers between devices, shards(): lax.all_to_all(x, 'row', split_axis=0, concat_axis=0, tiled=True)  50.3 us
    ppermute x11, waiting for transfers between devices, shards(): lax.ppermute(x, 'col', [(i, i ^ bits) for i in range(col_count)])  28.5 us
    pallas_call x3, Pallas kernels, tile_and_product(): pl.pallas_call(kernel, grid_spec=pltpu.PrefetchScalarGridSpec(num_scalar_...  23.8 us
    pallas_call x1, Pallas kernels, group_columns(): pl.pallas_call(kernel, grid=(steps + outs,), in_specs=[pl.BlockSpec((1, 1...  17.9 us
    pallas_call x1, Pallas kernels, group_rows(): pl.pallas_call(kernel, grid=(steps + outs,), in_specs=[pl.BlockSpec((1, 1...  16.9 us
    ppermute x11, starting transfers between devices, shards(): lax.ppermute(x, 'col', [(i, i ^ bits) for i in range(col_count)])  14.9 us
    all_to_all x3, starting transfers between devices, shards(): lax.all_to_all(x, 'row', split_axis=0, concat_axis=0, tiled=True)  12.4 us
  transfers between devices with their start and end apart: 15, of which 7 were waited for; matrix products, arithmetic and copies ran while one was open for 4% of the time, Pallas kernels for 5%

profile of v5, /device:TPU:0, one launch (start us, length us, event | category | flops | bytes accessed | tf_op | source)
XLA Modules:
  0.0 286.3 jit_solution(273645245701033475)
XLA Ops:
  0.6 1.1 fusion.18
  1.8 0.0 copy-start.3
  1.8 2.8 copy-done.3
  4.6 17.9 %group_columns.1 = f32[128,104,128]{2,1,0:T(8,128)S(1)} custom-call(s32[8,1,1792]{2,1,0:T(1,128)S(1)} %bitcast.18, f32[112,14336]{1,0:T(8,128)S(1)} %copy-done.3), custom_call_target="tpu_custom_call" | custom-call | tf_op jit(solution)/shard_map/group_columns/pallas_call | solution.py:55
  22.5 91.3 %all_to_all.25.x_ref = f32[128,104,128]{2,1,0:T(8,128)S(1)} all-to-all(f32[128,104,128]{2,1,0:T(8,128)S(1)} %group_columns.1), channel_id=1, replica_groups=mesh['row'=8,'col'=16] {'row','col'}, dimensions={0} | all-to-all | bytes 13631488 | tf_op jit(solution)/shard_map/all_to_all | solution.py:238
  113.8 16.9 %group_rows.1 = (f32[8,112,768]{2,1,0:T(8,128)}, f32[8,112,640]{2,1,0:T(8,128)S(1)}, f32[8,112,384]{2,1,0:T(8,128)S(1)}) custom-call(s32[8,1,1792]{2,1,0:T(1,128)S(1)} %bitcast.17, f32[128,104,128]{2,1,0:T(8,128)S(1)} %all_to_all.25.x_ref), custom_call_target="tpu_custom_call" | custom-call | tf_op jit(solution)/shard_map/group_rows/pallas_call | solution.py:114
  130.7 1.4 copy-done.4
  132.2 1.1 copy-done.6
  133.3 4.4 %all-to-all-start.1 = ((f32[8,112,768]{2,1,0:T(8,128)}), f32[8,112,768]{2,1,0:T(8,128)}, u32[]{:S(2)}, u32[]{:S(2)}) async-start(f32[8,112,768]{2,1,0:T(8,128)} %get-tuple-element.22), calls=%async_computation.1 | async-start | bytes 5505024 | tf_op jit(solution)/shard_map/all_to_all | solution.py:232
  137.7 0.1 pad_add_fusion.1
  137.8 4.2 %fusion = (bf16[896,1024]{1,0:T(8,128)(2,1)S(1)}, bf16[896,1024]{1,0:T(8,128)(2,1)}) fusion(f32[896,1024]{1,0:T(8,128)} %param.5), kind=kLoop, calls=%fused_computation.2 | loop fusion | flops 3670016 | bytes 7340032 | tf_op jit(solution)/shard_map/convert_element_type | solution.py:240
  141.9 29.9 %all-to-all-done.1.x_ref = f32[8,112,768]{2,1,0:T(8,128)} async-done(((f32[8,112,768]{2,1,0:T(8,128)}), f32[8,112,768]{2,1,0:T(8,128)}, u32[]{:S(2)}, u32[]{:S(2)}) %all-to-all-start.1) | async-done | bytes 2752544 | tf_op jit(solution)/shard_map/all_to_all | solution.py:232
  171.8 4.4 %all-to-all-start.2 = ((f32[8,112,640]{2,1,0:T(8,128)}), f32[8,112,640]{2,1,0:T(8,128)}, u32[]{:S(2)}, u32[]{:S(2)}) async-start(f32[8,112,640]{2,1,0:T(8,128)} %copy-done.4), calls=%async_computation.2 | async-start | bytes 4587520 | tf_op jit(solution)/shard_map/all_to_all | solution.py:232
  176.2 1.5 copy-done
  177.7 9.6 %shard_map.50 = (f32[16,112,896]{2,1,0:T(8,128)}, f32[8,48,1024]{2,1,0:T(8,128)S(1)}, f32[8,48,1024]{2,1,0:T(8,128)S(1)}) custom-call(s32[3]{0:T(128)S(1)} %get-tuple-element.47.where_ref, f32[8,112,768]{2,1,0:T(8,128)} %all-to-all-done.1.x_ref, bf16[896,1024]{1,0:T(8,128)(2,1)S(1)} %copy-done, bf16[896,1024]{1,0:T(8,128)(2,1)S(1)} %get-tuple-element.36.lo_ref), custom_call_target="tpu_custom_call" | custom-call | flops 4227858432 | bytes 5505024 | tf_op jit(solution)/shard_map/pallas_call | solution.py:187
  187.4 0.1 collective-permute-start
  187.5 3.4 %collective-permute-done = f32[8,48,1024]{2,1,0:T(8,128)S(1)} collective-permute-done((f32[8,48,1024]{2,1,0:T(8,128)S(1)}, f32[8,48,1024]{2,1,0:T(8,128)S(1)}, u32[]{:S(2)}, u32[]{:S(2)}) %collective-permute-start) | collective-permute-done | bytes 1572896 | tf_op jit(solution)/shard_map/ppermute | solution.py:233
  190.9 1.1 copy-done.8
  192.0 1.1 slice_add_fusion.1
  193.1 11.5 %all-to-all-done.2.x_ref = f32[8,112,640]{2,1,0:T(8,128)} async-done(((f32[8,112,640]{2,1,0:T(8,128)}), f32[8,112,640]{2,1,0:T(8,128)}, u32[]{:S(2)}, u32[]{:S(2)}) %all-to-all-start.2) | async-done | bytes 2293792 | tf_op jit(solution)/shard_map/all_to_all | solution.py:232
  204.6 1.5 copy-done.1
  206.1 9.1 %shard_map.51 = (f32[16,112,896]{2,1,0:T(8,128)}, f32[8,40,1024]{2,1,0:T(8,128)}, f32[8,40,1024]{2,1,0:T(8,128)S(1)}) custom-call(s32[3]{0:T(128)S(1)} %get-tuple-element.46.where_ref, f32[8,112,640]{2,1,0:T(8,128)} %all-to-all-done.2.x_ref, bf16[896,1024]{1,0:T(8,128)(2,1)S(1)} %copy-done.1, ...), custom_call_target="tpu_custom_call", output_to_operand_aliasing={{0}: (4, {})} | custom-call | flops 3523215360 | bytes 4587520 | tf_op jit(solution)/shard_map/pallas_call | solution.py:187
  215.2 1.1 copy-done.7
  216.3 0.0 collective-permute-start.1
  216.3 3.6 %all-to-all-start.3 = ((f32[8,112,384]{2,1,0:T(8,128)}), f32[8,112,384]{2,1,0:T(8,128)S(1)}, u32[]{:S(2)}, u32[]{:S(2)}) async-start(f32[8,112,384]{2,1,0:T(8,128)} %copy-done.6), calls=%async_computation.3 | async-start | bytes 2752512 | tf_op jit(solution)/shard_map/all_to_all | solution.py:232
  219.9 0.1 pad_add_fusion.where_ref
  220.0 0.0 collective-permute-start.2
  220.0 4.0 %collective-permute-start.3 = (f32[2,48,1024]{2,1,0:T(8,128)}, f32[2,48,1024]{2,1,0:T(8,128)}, u32[]{:S(2)}, u32[]{:S(2)}) collective-permute-start(f32[2,48,1024]{2,1,0:T(8,128)} %get-tuple-element.39), channel_id=1, source_target_pairs={{0,8},{1,9},{2,10},{3,11},{4,12},{5,13},{6,14},{7,15},{8,0},{9,1},... | collective-permute-start | bytes 1179656 | tf_op jit(solution)/shard_map/ppermute | solution.py:233
  224.0 0.7 collective-permute-start.4
  224.7 0.0 collective-permute-done.1
  224.7 2.5 slice_add_fusion.5
  227.2 0.6 collective-permute-start.6
  227.8 3.4 %collective-permute-start.7 = (f32[2,40,1024]{2,1,0:T(8,128)}, f32[2,40,1024]{2,1,0:T(8,128)}, u32[]{:S(2)}, u32[]{:S(2)}) collective-permute-start(f32[2,40,1024]{2,1,0:T(8,128)} %get-tuple-element.42), channel_id=1, source_target_pairs={{0,8},{1,9},{2,10},{3,11},{4,12},{5,13},{6,14},{7,15},{8,0},{9,1},... | collective-permute-start | bytes 983048 | tf_op jit(solution)/shard_map/ppermute | solution.py:233
  231.1 8.9 %all-to-all-done.3.x_ref = f32[8,112,384]{2,1,0:T(8,128)S(1)} async-done(((f32[8,112,384]{2,1,0:T(8,128)}), f32[8,112,384]{2,1,0:T(8,128)S(1)}, u32[]{:S(2)}, u32[]{:S(2)}) %all-to-all-start.3) | async-done | bytes 1376288 | tf_op jit(solution)/shard_map/all_to_all | solution.py:232
  240.0 1.5 copy-done.2
  241.5 5.0 %shard_map.52 = (f32[16,112,896]{2,1,0:T(8,128)}, f32[8,24,1024]{2,1,0:T(8,128)S(1)}, f32[8,24,1024]{2,1,0:T(8,128)S(1)}) custom-call(s32[3]{0:T(128)S(1)} %pad_add_fusion.where_ref, f32[8,112,384]{2,1,0:T(8,128)S(1)} %all-to-all-done.3.x_ref, bf16[896,1024]{1,0:T(8,128)(2,1)S(1)} %copy-done.2, ...), custom_call_target="tpu_custom_call", output_to_operand_aliasing={{0}: (4, {})} | custom-call | flops 2113929216 | bytes 2752512 | tf_op jit(solution)/shard_map/pallas_call | solution.py:187
  246.6 0.0 collective-permute-done.2
  246.6 2.5 collective-permute-start.8
  249.1 1.6 fusion.3
  250.8 0.1 collective-permute-start.5
  250.9 5.7 %collective-permute-done.7 = f32[2,40,1024]{2,1,0:T(8,128)} collective-permute-done((f32[2,40,1024]{2,1,0:T(8,128)}, f32[2,40,1024]{2,1,0:T(8,128)}, u32[]{:S(2)}, u32[]{:S(2)}) %collective-permute-start.7) | collective-permute-done | bytes 327712 | tf_op jit(solution)/shard_map/ppermute | solution.py:233
  256.6 6.8 %collective-permute-done.8 = f32[2,40,1024]{2,1,0:T(8,128)S(1)} collective-permute-done((f32[2,40,1024]{2,1,0:T(8,128)S(1)}, f32[2,40,1024]{2,1,0:T(8,128)S(1)}, u32[]{:S(2)}, u32[]{:S(2)}) %collective-permute-start.8) | collective-permute-done | bytes 327712 | tf_op jit(solution)/shard_map/ppermute | solution.py:233
  263.4 1.3 fusion.6
  264.7 1.0 add.157
  265.7 3.5 %all-to-all-start.4 = ((f32[8,24,1024]{2,1,0:T(8,128)}), f32[8,24,1024]{2,1,0:T(8,128)S(1)}, u32[]{:S(2)}, u32[]{:S(2)}) async-start(f32[8,24,1024]{2,1,0:T(8,128)} %add.157), calls=%async_computation.4 | async-start | bytes 1572864 | tf_op jit(solution)/shard_map/all_to_all | solution.py:264
  269.3 3.5 %collective-permute-start.9 = (f32[40,1024]{1,0:T(8,128)S(1)}, f32[40,1024]{1,0:T(8,128)S(1)}, u32[]{:S(2)}, u32[]{:S(2)}) collective-permute-start(f32[40,1024]{1,0:T(8,128)S(1)} %slice_bitcast_fusion.2), channel_id=1, source_target_pairs={{0,2},{1,3},{2,0},{3,1},{4,6},{5,7},{6,4},{7,5},{8,10},{9,11},{10,... | collective-permute-start | bytes 491528 | tf_op jit(solution)/shard_map/ppermute | solution.py:233
  272.8 12.6 %collective-permute-done.9 = f32[40,1024]{1,0:T(8,128)S(1)} collective-permute-done((f32[40,1024]{1,0:T(8,128)S(1)}, f32[40,1024]{1,0:T(8,128)S(1)}, u32[]{:S(2)}, u32[]{:S(2)}) %collective-permute-start.9) | collective-permute-done | bytes 163872 | tf_op jit(solution)/shard_map/ppermute | solution.py:233
  285.5 0.8 pad_maximum_fusion
  (23 shorter events, 0.2 us)
Async XLA Ops:
  1.8 2.8 copy-start.3
  130.7 1.4 copy-start.4
  132.1 1.1 copy-start.6
  133.3 38.6 %all-to-all-start.1 = ((f32[8,112,768]{2,1,0:T(8,128)}), f32[8,112,768]{2,1,0:T(8,128)}, u32[]{:S(2)}, u32[]{:S(2)}) async-start(f32[8,112,768]{2,1,0:T(8,128)} %get-tuple-element.22), calls=%async_computation.1 | async-start | bytes 5505024 | tf_op jit(solution)/shard_map/all_to_all | solution.py:232
  171.8 32.7 %all-to-all-start.2 = ((f32[8,112,640]{2,1,0:T(8,128)}), f32[8,112,640]{2,1,0:T(8,128)}, u32[]{:S(2)}, u32[]{:S(2)}) async-start(f32[8,112,640]{2,1,0:T(8,128)} %copy-done.4), calls=%async_computation.2 | async-start | bytes 4587520 | tf_op jit(solution)/shard_map/all_to_all | solution.py:232
  176.2 1.5 copy-start
  187.4 3.5 %copy-start.5 = (f32[8,48,1024]{2,1,0:T(8,128)}, f32[8,48,1024]{2,1,0:T(8,128)S(1)}, u32[]{:S(2)}) copy-start(f32[8,48,1024]{2,1,0:T(8,128)S(1)} %get-tuple-element.25) | copy-start | bytes 4718596
  187.4 3.5 %collective-permute-start = (f32[8,48,1024]{2,1,0:T(8,128)S(1)}, f32[8,48,1024]{2,1,0:T(8,128)S(1)}, u32[]{:S(2)}, u32[]{:S(2)}) collective-permute-start(f32[8,48,1024]{2,1,0:T(8,128)S(1)} %get-tuple-element.26), channel_id=1, source_target_pairs={{0,1},{1,0},{2,3},{3,2},{4,5},{5,4},{6,7},{7,6},{8,9},{9,8},{10,11... | collective-permute-start | bytes 4718600 | tf_op jit(solution)/shard_map/ppermute | solution.py:233
  190.9 1.1 copy-start.8
  204.6 1.5 copy-start.1
  215.2 1.1 copy-start.7
  216.3 8.4 %collective-permute-start.1 = (f32[8,40,1024]{2,1,0:T(8,128)}, f32[8,40,1024]{2,1,0:T(8,128)}, u32[]{:S(2)}, u32[]{:S(2)}) collective-permute-start(f32[8,40,1024]{2,1,0:T(8,128)} %get-tuple-element.30), channel_id=1, source_target_pairs={{0,1},{1,0},{2,3},{3,2},{4,5},{5,4},{6,7},{7,6},{8,9},{9,8},{10,11... | collective-permute-start | bytes 3932168 | tf_op jit(solution)/shard_map/ppermute | solution.py:233
  216.3 23.7 %all-to-all-start.3 = ((f32[8,112,384]{2,1,0:T(8,128)}), f32[8,112,384]{2,1,0:T(8,128)S(1)}, u32[]{:S(2)}, u32[]{:S(2)}) async-start(f32[8,112,384]{2,1,0:T(8,128)} %copy-done.6), calls=%async_computation.3 | async-start | bytes 2752512 | tf_op jit(solution)/shard_map/all_to_all | solution.py:232
  220.0 26.6 %collective-permute-start.2 = (f32[2,48,1024]{2,1,0:T(8,128)}, f32[2,48,1024]{2,1,0:T(8,128)}, u32[]{:S(2)}, u32[]{:S(2)}) collective-permute-start(f32[2,48,1024]{2,1,0:T(8,128)} %get-tuple-element.40), channel_id=1, source_target_pairs={{0,4},{1,5},{2,6},{3,7},{4,0},{5,1},{6,2},{7,3},{8,12},{9,13},{10,... | collective-permute-start | bytes 1179656 | tf_op jit(solution)/shard_map/ppermute | solution.py:233
  220.0 29.1 %collective-permute-start.3 = (f32[2,48,1024]{2,1,0:T(8,128)}, f32[2,48,1024]{2,1,0:T(8,128)}, u32[]{:S(2)}, u32[]{:S(2)}) collective-permute-start(f32[2,48,1024]{2,1,0:T(8,128)} %get-tuple-element.39), channel_id=1, source_target_pairs={{0,8},{1,9},{2,10},{3,11},{4,12},{5,13},{6,14},{7,15},{8,0},{9,1},... | collective-permute-start | bytes 1179656 | tf_op jit(solution)/shard_map/ppermute | solution.py:233
  224.0 25.2 %collective-permute-start.4 = (f32[2,48,1024]{2,1,0:T(8,128)}, f32[2,48,1024]{2,1,0:T(8,128)}, u32[]{:S(2)}, u32[]{:S(2)}) collective-permute-start(f32[2,48,1024]{2,1,0:T(8,128)} %get-tuple-element.38), channel_id=1, source_target_pairs={{0,12},{1,13},{2,14},{3,15},{4,8},{5,9},{6,10},{7,11},{8,4},{9,5},... | collective-permute-start | bytes 1179656 | tf_op jit(solution)/shard_map/ppermute | solution.py:233
  227.2 23.7 %collective-permute-start.6 = (f32[2,40,1024]{2,1,0:T(8,128)}, f32[2,40,1024]{2,1,0:T(8,128)S(1)}, u32[]{:S(2)}, u32[]{:S(2)}) collective-permute-start(f32[2,40,1024]{2,1,0:T(8,128)} %get-tuple-element.43), channel_id=1, source_target_pairs={{0,4},{1,5},{2,6},{3,7},{4,0},{5,1},{6,2},{7,3},{8,12},{9,13},{10,... | collective-permute-start | bytes 983048 | tf_op jit(solution)/shard_map/ppermute | solution.py:233
  227.8 28.8 %collective-permute-start.7 = (f32[2,40,1024]{2,1,0:T(8,128)}, f32[2,40,1024]{2,1,0:T(8,128)}, u32[]{:S(2)}, u32[]{:S(2)}) collective-permute-start(f32[2,40,1024]{2,1,0:T(8,128)} %get-tuple-element.42), channel_id=1, source_target_pairs={{0,8},{1,9},{2,10},{3,11},{4,12},{5,13},{6,14},{7,15},{8,0},{9,1},... | collective-permute-start | bytes 983048 | tf_op jit(solution)/shard_map/ppermute | solution.py:233
  240.0 1.5 copy-start.2
  241.5 5.1 %copy-start.9 = (f32[2,40,1024]{2,1,0:T(8,128)S(1)}, f32[2,40,1024]{2,1,0:T(8,128)}, u32[]{:S(2)}) copy-start(f32[2,40,1024]{2,1,0:T(8,128)} %get-tuple-element.41) | copy-start | bytes 983044
  246.6 16.8 %collective-permute-start.8 = (f32[2,40,1024]{2,1,0:T(8,128)S(1)}, f32[2,40,1024]{2,1,0:T(8,128)S(1)}, u32[]{:S(2)}, u32[]{:S(2)}) collective-permute-start(f32[2,40,1024]{2,1,0:T(8,128)S(1)} %copy-done.9), channel_id=1, source_target_pairs={{0,12},{1,13},{2,14},{3,15},{4,8},{5,9},{6,10},{7,11},{8,4},{9,5},... | collective-permute-start | bytes 983048 | tf_op jit(solution)/shard_map/ppermute | solution.py:233
  249.1 15.6 %collective-permute-start.10 = (f32[8,24,1024]{2,1,0:T(8,128)S(1)}, f32[8,24,1024]{2,1,0:T(8,128)S(1)}, u32[]{:S(2)}, u32[]{:S(2)}) collective-permute-start(f32[8,24,1024]{2,1,0:T(8,128)S(1)} %get-tuple-element.35), channel_id=1, source_target_pairs={{0,1},{1,0},{2,3},{3,2},{4,5},{5,4},{6,7},{7,6},{8,9},{9,8},{10,11... | collective-permute-start | bytes 2359304 | tf_op jit(solution)/shard_map/ppermute | solution.py:233
  250.8 22.0 %collective-permute-start.5 = (f32[48,1024]{1,0:T(8,128)S(1)}, f32[48,1024]{1,0:T(8,128)S(1)}, u32[]{:S(2)}, u32[]{:S(2)}) collective-permute-start(f32[48,1024]{1,0:T(8,128)S(1)} %slice_bitcast_fusion), channel_id=1, source_target_pairs={{0,2},{1,3},{2,0},{3,1},{4,6},{5,7},{6,4},{7,5},{8,10},{9,11},{10,... | collective-permute-start | bytes 589832 | tf_op jit(solution)/shard_map/ppermute | solution.py:233
  265.7 19.7 %all-to-all-start.4 = ((f32[8,24,1024]{2,1,0:T(8,128)}), f32[8,24,1024]{2,1,0:T(8,128)S(1)}, u32[]{:S(2)}, u32[]{:S(2)}) async-start(f32[8,24,1024]{2,1,0:T(8,128)} %add.157), calls=%async_computation.4 | async-start | bytes 1572864 | tf_op jit(solution)/shard_map/all_to_all | solution.py:264
  269.3 16.1 %collective-permute-start.9 = (f32[40,1024]{1,0:T(8,128)S(1)}, f32[40,1024]{1,0:T(8,128)S(1)}, u32[]{:S(2)}, u32[]{:S(2)}) collective-permute-start(f32[40,1024]{1,0:T(8,128)S(1)} %slice_bitcast_fusion.2), channel_id=1, source_target_pairs={{0,2},{1,3},{2,0},{3,1},{4,6},{5,7},{6,4},{7,5},{8,10},{9,11},{10,... | collective-permute-start | bytes 491528 | tf_op jit(solution)/shard_map/ppermute | solution.py:233

commit v6 on v5

--- a/solution.py
+++ b/solution.py
@@ -123,7 +123,7 @@
             pltpu.VMEM((per * SUB, LANES), jnp.float32),
             pltpu.VMEM((unknowns, LANES), jnp.float32),
         ],
-        out_shape=[jax.ShapeDtypeStruct((groups, share, w), jnp.float32) for w in widths],
+        out_shape=[(pltpu.HBM if i else jax.ShapeDtypeStruct)((groups, share, w), jnp.float32) for i, w in enumerate(widths)],
         compiler_params=params(),
         name="group_rows",
     )(places, blocks)
@@ -234,7 +234,8 @@
     groups = [list(range(p, col_count, 2)) for p in range(2)]
     widths = [s * col_count for s in SPANS]
 
-    outgoing = group_columns(normal_matrix, column_places, devices)
+    in_hbm = lambda x: pltpu.with_memory_space_constraint(x, pltpu.HBM)
+    outgoing = group_columns(in_hbm(normal_matrix), column_places, devices)
     arrived = lax.all_to_all(outgoing, ("row", "col"), split_axis=0, concat_axis=0, tiled=True)
     v_hi = lax.reduce_precision(check_vectors, 8, 7)
     v_lo = (check_vectors - v_hi).astype(jnp.bfloat16)
@@ -256,7 +257,9 @@
             piece, _ = lax.optimization_barrier((last, held))
         turn = me // 2 if not final else me * 0
         where = jnp.stack([me % 2, turn, me * 0 + q])
-        tile_layout, other, mine = tile_and_product(piece, v_hi, v_lo, where, tile_layout, col_count, share, offset)
+        tile_layout, other, mine = tile_and_product(
+            piece, in_hbm(v_hi), in_hbm(v_lo), where, tile_layout, col_count, share, offset
+        )
         offset += span
         theirs = flip(other, 1)
         if final:

time: 287 us -> 281 us (0.979)
  local copies, waits for them, and re-layouts: 12.1 us -> 2.78 us
    unnamed x20 -> x8, local copies, waits for them, and re-layouts: 12 us -> 2.75 us
where the time goes in v6:
time: 281 us; the launch traced here: 280 us
  blocking collectives  91.3 us (32%)
  waiting for transfers between devices  81.2 us (29%)
  Pallas kernels  60.1 us (21%)
  starting transfers between devices  30.1 us (11%)
  other arithmetic  13.9 us (5%)
    all_to_all x1, blocking collectives, shards(): lax.all_to_all(outgoing, ('row', 'col'), split_axis=0, concat_axis=0, til...  91.3 us
    all_to_all x3, waiting for transfers between devices, shards(): lax.all_to_all(x, 'row', split_axis=0, concat_axis=0, tiled=True)  52.2 us
    ppermute x11, waiting for transfers between devices, shards(): lax.ppermute(x, 'col', [(i, i ^ bits) for i in range(col_count)])  29 us
    pallas_call x3, Pallas kernels, tile_and_product(): pl.pallas_call(kernel, grid_spec=pltpu.PrefetchScalarGridSpec(num_scalar_...  24.8 us
    pallas_call x1, Pallas kernels, group_columns(): pl.pallas_call(kernel, grid=(steps + outs,), in_specs=[pl.BlockSpec((1, 1...  18.1 us
    pallas_call x1, Pallas kernels, group_rows(): pl.pallas_call(kernel, grid=(steps + outs,), in_specs=[pl.BlockSpec((1, 1...  17.1 us
    ppermute x11, starting transfers between devices, shards(): lax.ppermute(x, 'col', [(i, i ^ bits) for i in range(col_count)])  15 us
    all_to_all x3, starting transfers between devices, shards(): lax.all_to_all(x, 'row', split_axis=0, concat_axis=0, tiled=True)  11.6 us
  transfers between devices with their start and end apart: 15, of which 7 were waited for; matrix products, arithmetic and copies ran while one was open for 4% of the time, Pallas kernels for 5%

profile of v6, /device:TPU:0, one launch (start us, length us, event | category | flops | bytes accessed | tf_op | source)
XLA Modules:
  0.0 280.3 jit_solution(15993044388461339146)
XLA Ops:
  0.6 1.1 fusion.18
  1.8 18.1 %group_columns.1 = f32[128,104,128]{2,1,0:T(8,128)S(1)} custom-call(s32[8,1,1792]{2,1,0:T(1,128)S(1)} %bitcast.18, f32[112,14336]{1,0:T(8,128)} %x_ref.1), custom_call_target="tpu_custom_call" | custom-call | tf_op jit(solution)/shard_map/group_columns/pallas_call | solution.py:55
  19.9 91.3 %all_to_all.25.x_ref = f32[128,104,128]{2,1,0:T(8,128)S(1)} all-to-all(f32[128,104,128]{2,1,0:T(8,128)S(1)} %group_columns.1), channel_id=1, replica_groups=mesh['row'=8,'col'=16] {'row','col'}, dimensions={0} | all-to-all | bytes 13631488 | tf_op jit(solution)/shard_map/all_to_all | solution.py:239
  111.2 17.1 %group_rows.1 = (f32[8,112,768]{2,1,0:T(8,128)S(1)}, f32[8,112,640]{2,1,0:T(8,128)}, f32[8,112,384]{2,1,0:T(8,128)}) custom-call(s32[8,1,1792]{2,1,0:T(1,128)S(1)} %bitcast.17, f32[128,104,128]{2,1,0:T(8,128)S(1)} %all_to_all.25.x_ref), custom_call_target="tpu_custom_call" | custom-call | tf_op jit(solution)/shard_map/group_rows/pallas_call | solution.py:114
  128.4 1.5 copy-done
  129.9 3.6 %all-to-all-start.1 = ((f32[8,112,768]{2,1,0:T(8,128)}), f32[8,112,768]{2,1,0:T(8,128)S(1)}, u32[]{:S(2)}, u32[]{:S(2)}) async-start(f32[8,112,768]{2,1,0:T(8,128)} %copy-done), calls=%async_computation.1 | async-start | bytes 5505024 | tf_op jit(solution)/shard_map/all_to_all | solution.py:232
  133.5 0.1 pad_add_fusion.1
  133.6 4.7 %fusion = (bf16[896,1024]{1,0:T(8,128)(2,1)}, bf16[896,1024]{1,0:T(8,128)(2,1)}) fusion(f32[896,1024]{1,0:T(8,128)} %param.5), kind=kLoop, calls=%fused_computation.2 | loop fusion | flops 3670016 | bytes 7340032 | tf_op jit(solution)/shard_map/convert_element_type | solution.py:241
  138.4 29.2 %all-to-all-done.1.x_ref = f32[8,112,768]{2,1,0:T(8,128)S(1)} async-done(((f32[8,112,768]{2,1,0:T(8,128)}), f32[8,112,768]{2,1,0:T(8,128)S(1)}, u32[]{:S(2)}, u32[]{:S(2)}) %all-to-all-start.1) | async-done | bytes 2752544 | tf_op jit(solution)/shard_map/all_to_all | solution.py:232
  167.6 4.4 %all-to-all-start.2 = ((f32[8,112,640]{2,1,0:T(8,128)}), f32[8,112,640]{2,1,0:T(8,128)}, u32[]{:S(2)}, u32[]{:S(2)}) async-start(f32[8,112,640]{2,1,0:T(8,128)} %get-tuple-element.23), calls=%async_computation.2 | async-start | bytes 4587520 | tf_op jit(solution)/shard_map/all_to_all | solution.py:232
  172.0 8.9 %shard_map.50 = (f32[16,112,896]{2,1,0:T(8,128)}, f32[8,48,1024]{2,1,0:T(8,128)S(1)}, f32[8,48,1024]{2,1,0:T(8,128)S(1)}) custom-call(s32[3]{0:T(128)S(1)} %get-tuple-element.47.where_ref, f32[8,112,768]{2,1,0:T(8,128)S(1)} %all-to-all-done.1.x_ref, bf16[896,1024]{1,0:T(8,128)(2,1)} %get-tuple-element.37.hi_ref, bf16[896,1024]{1,0:T(8,128)(2,1)} %get-tuple-element.36.lo_ref), custom_call_target="tpu_custom_call" | custom-call | flops 4227858432 | bytes 5505024 | tf_op jit(solution)/shard_map/pallas_call | solution.py:187
  180.9 0.1 collective-permute-start
  181.0 3.4 %collective-permute-done = f32[8,48,1024]{2,1,0:T(8,128)S(1)} collective-permute-done((f32[8,48,1024]{2,1,0:T(8,128)S(1)}, f32[8,48,1024]{2,1,0:T(8,128)S(1)}, u32[]{:S(2)}, u32[]{:S(2)}) %collective-permute-start) | collective-permute-done | bytes 1572896 | tf_op jit(solution)/shard_map/ppermute | solution.py:233
  184.4 1.2 copy-done.2
  185.6 1.0 slice_add_fusion.1
  186.6 13.8 %all-to-all-done.2.x_ref = f32[8,112,640]{2,1,0:T(8,128)} async-done(((f32[8,112,640]{2,1,0:T(8,128)}), f32[8,112,640]{2,1,0:T(8,128)}, u32[]{:S(2)}, u32[]{:S(2)}) %all-to-all-start.2) | async-done | bytes 2293792 | tf_op jit(solution)/shard_map/all_to_all | solution.py:232
  200.3 9.9 %shard_map.51 = (f32[16,112,896]{2,1,0:T(8,128)}, f32[8,40,1024]{2,1,0:T(8,128)}, f32[8,40,1024]{2,1,0:T(8,128)S(1)}) custom-call(s32[3]{0:T(128)S(1)} %get-tuple-element.46.where_ref, f32[8,112,640]{2,1,0:T(8,128)} %all-to-all-done.2.x_ref, bf16[896,1024]{1,0:T(8,128)(2,1)} %get-tuple-element.37.hi_ref, ...), custom_call_target="tpu_custom_call", output_to_operand_aliasing={{0}: (4, {})} | custom-call | flops 3523215360 | bytes 4587520 | tf_op jit(solution)/shard_map/pallas_call | solution.py:187
  210.2 0.1 collective-permute-start.1
  210.3 3.6 %all-to-all-start.3 = ((f32[8,112,384]{2,1,0:T(8,128)}), f32[8,112,384]{2,1,0:T(8,128)S(1)}, u32[]{:S(2)}, u32[]{:S(2)}) async-start(f32[8,112,384]{2,1,0:T(8,128)} %get-tuple-element.24), calls=%async_computation.3 | async-start | bytes 2752512 | tf_op jit(solution)/shard_map/all_to_all | solution.py:232
  213.9 0.1 pad_add_fusion.where_ref
  214.0 0.0 collective-permute-start.2
  214.0 4.0 %collective-permute-start.3 = (f32[2,48,1024]{2,1,0:T(8,128)S(1)}, f32[2,48,1024]{2,1,0:T(8,128)}, u32[]{:S(2)}, u32[]{:S(2)}) collective-permute-start(f32[2,48,1024]{2,1,0:T(8,128)S(1)} %get-tuple-element.39), channel_id=1, source_target_pairs={{0,8},{1,9},{2,10},{3,11},{4,12},{5,13},{6,14},{7,15},{8,0},{9,1},... | collective-permute-start | bytes 1179656 | tf_op jit(solution)/shard_map/ppermute | solution.py:233
  218.0 0.7 collective-permute-start.4
  218.7 0.0 collective-permute-done.1
  218.7 2.1 slice_add_fusion.5
  220.9 0.6 collective-permute-start.6
  221.5 3.4 %collective-permute-start.7 = (f32[2,40,1024]{2,1,0:T(8,128)}, f32[2,40,1024]{2,1,0:T(8,128)}, u32[]{:S(2)}, u32[]{:S(2)}) collective-permute-start(f32[2,40,1024]{2,1,0:T(8,128)} %get-tuple-element.42), channel_id=1, source_target_pairs={{0,8},{1,9},{2,10},{3,11},{4,12},{5,13},{6,14},{7,15},{8,0},{9,1},... | collective-permute-start | bytes 983048 | tf_op jit(solution)/shard_map/ppermute | solution.py:233
  224.8 9.2 %all-to-all-done.3.x_ref = f32[8,112,384]{2,1,0:T(8,128)S(1)} async-done(((f32[8,112,384]{2,1,0:T(8,128)}), f32[8,112,384]{2,1,0:T(8,128)S(1)}, u32[]{:S(2)}, u32[]{:S(2)}) %all-to-all-start.3) | async-done | bytes 1376288 | tf_op jit(solution)/shard_map/all_to_all | solution.py:232
  234.0 6.1 %shard_map.52 = (f32[16,112,896]{2,1,0:T(8,128)}, f32[8,24,1024]{2,1,0:T(8,128)S(1)}, f32[8,24,1024]{2,1,0:T(8,128)S(1)}) custom-call(s32[3]{0:T(128)S(1)} %pad_add_fusion.where_ref, f32[8,112,384]{2,1,0:T(8,128)S(1)} %all-to-all-done.3.x_ref, bf16[896,1024]{1,0:T(8,128)(2,1)} %get-tuple-element.37.hi_ref, ...), custom_call_target="tpu_custom_call", output_to_operand_aliasing={{0}: (4, {})} | custom-call | flops 2113929216 | bytes 2752512 | tf_op jit(solution)/shard_map/pallas_call | solution.py:187
  240.1 0.0 collective-permute-done.2
  240.1 2.5 collective-permute-start.8
  242.7 0.0 collective-permute-done.3
  242.7 0.0 collective-permute-start.10
  242.7 0.0 collective-permute-done.4
  242.7 1.6 fusion.3
  244.3 0.1 collective-permute-start.5
  244.4 0.0 collective-permute-done.6
  244.4 6.1 %collective-permute-done.7 = f32[2,40,1024]{2,1,0:T(8,128)} collective-permute-done((f32[2,40,1024]{2,1,0:T(8,128)}, f32[2,40,1024]{2,1,0:T(8,128)}, u32[]{:S(2)}, u32[]{:S(2)}) %collective-permute-start.7) | collective-permute-done | bytes 327712 | tf_op jit(solution)/shard_map/ppermute | solution.py:233
  250.6 6.8 %collective-permute-done.8 = f32[2,40,1024]{2,1,0:T(8,128)S(1)} collective-permute-done((f32[2,40,1024]{2,1,0:T(8,128)S(1)}, f32[2,40,1024]{2,1,0:T(8,128)S(1)}, u32[]{:S(2)}, u32[]{:S(2)}) %collective-permute-start.8) | collective-permute-done | bytes 327712 | tf_op jit(solution)/shard_map/ppermute | solution.py:233
  257.4 1.3 fusion.6
  258.7 0.0 collective-permute-done.10
  258.7 1.0 add.157
  259.7 3.5 %all-to-all-start.4 = ((f32[8,24,1024]{2,1,0:T(8,128)}), f32[8,24,1024]{2,1,0:T(8,128)S(1)}, u32[]{:S(2)}, u32[]{:S(2)}) async-start(f32[8,24,1024]{2,1,0:T(8,128)} %add.157), calls=%async_computation.4 | async-start | bytes 1572864 | tf_op jit(solution)/shard_map/all_to_all | solution.py:267
  263.3 3.5 %collective-permute-start.9 = (f32[40,1024]{1,0:T(8,128)S(1)}, f32[40,1024]{1,0:T(8,128)S(1)}, u32[]{:S(2)}, u32[]{:S(2)}) collective-permute-start(f32[40,1024]{1,0:T(8,128)S(1)} %slice_bitcast_fusion.2), channel_id=1, source_target_pairs={{0,2},{1,3},{2,0},{3,1},{4,6},{5,7},{6,4},{7,5},{8,10},{9,11},{10,... | collective-permute-start | bytes 491528 | tf_op jit(solution)/shard_map/ppermute | solution.py:233
  266.8 0.0 collective-permute-done.5
  266.8 12.6 %collective-permute-done.9 = f32[40,1024]{1,0:T(8,128)S(1)} collective-permute-done((f32[40,1024]{1,0:T(8,128)S(1)}, f32[40,1024]{1,0:T(8,128)S(1)}, u32[]{:S(2)}, u32[]{:S(2)}) %collective-permute-start.9) | collective-permute-done | bytes 163872 | tf_op jit(solution)/shard_map/ppermute | solution.py:233
  279.4 0.0 all-to-all-done.4
  279.5 0.8 pad_maximum_fusion
  (11 shorter events, 0.1 us)
Async XLA Ops:
  128.3 1.5 copy-start
  129.9 37.7 %all-to-all-start.1 = ((f32[8,112,768]{2,1,0:T(8,128)}), f32[8,112,768]{2,1,0:T(8,128)S(1)}, u32[]{:S(2)}, u32[]{:S(2)}) async-start(f32[8,112,768]{2,1,0:T(8,128)} %copy-done), calls=%async_computation.1 | async-start | bytes 5505024 | tf_op jit(solution)/shard_map/all_to_all | solution.py:232
  167.6 32.8 %all-to-all-start.2 = ((f32[8,112,640]{2,1,0:T(8,128)}), f32[8,112,640]{2,1,0:T(8,128)}, u32[]{:S(2)}, u32[]{:S(2)}) async-start(f32[8,112,640]{2,1,0:T(8,128)} %get-tuple-element.23), calls=%async_computation.2 | async-start | bytes 4587520 | tf_op jit(solution)/shard_map/all_to_all | solution.py:232
  180.9 3.5 %copy-start.1 = (f32[8,48,1024]{2,1,0:T(8,128)}, f32[8,48,1024]{2,1,0:T(8,128)S(1)}, u32[]{:S(2)}) copy-start(f32[8,48,1024]{2,1,0:T(8,128)S(1)} %get-tuple-element.25) | copy-start | bytes 4718596
  180.9 3.5 %collective-permute-start = (f32[8,48,1024]{2,1,0:T(8,128)S(1)}, f32[8,48,1024]{2,1,0:T(8,128)S(1)}, u32[]{:S(2)}, u32[]{:S(2)}) collective-permute-start(f32[8,48,1024]{2,1,0:T(8,128)S(1)} %get-tuple-element.26), channel_id=1, source_target_pairs={{0,1},{1,0},{2,3},{3,2},{4,5},{5,4},{6,7},{7,6},{8,9},{9,8},{10,11... | collective-permute-start | bytes 4718600 | tf_op jit(solution)/shard_map/ppermute | solution.py:233
  184.4 1.2 copy-start.2
  210.2 8.5 %collective-permute-start.1 = (f32[8,40,1024]{2,1,0:T(8,128)}, f32[8,40,1024]{2,1,0:T(8,128)}, u32[]{:S(2)}, u32[]{:S(2)}) collective-permute-start(f32[8,40,1024]{2,1,0:T(8,128)} %get-tuple-element.30), channel_id=1, source_target_pairs={{0,1},{1,0},{2,3},{3,2},{4,5},{5,4},{6,7},{7,6},{8,9},{9,8},{10,11... | collective-permute-start | bytes 3932168 | tf_op jit(solution)/shard_map/ppermute | solution.py:233
  210.3 23.7 %all-to-all-start.3 = ((f32[8,112,384]{2,1,0:T(8,128)}), f32[8,112,384]{2,1,0:T(8,128)S(1)}, u32[]{:S(2)}, u32[]{:S(2)}) async-start(f32[8,112,384]{2,1,0:T(8,128)} %get-tuple-element.24), calls=%async_computation.3 | async-start | bytes 2752512 | tf_op jit(solution)/shard_map/all_to_all | solution.py:232
  214.0 26.1 %collective-permute-start.2 = (f32[2,48,1024]{2,1,0:T(8,128)}, f32[2,48,1024]{2,1,0:T(8,128)}, u32[]{:S(2)}, u32[]{:S(2)}) collective-permute-start(f32[2,48,1024]{2,1,0:T(8,128)} %get-tuple-element.40), channel_id=1, source_target_pairs={{0,4},{1,5},{2,6},{3,7},{4,0},{5,1},{6,2},{7,3},{8,12},{9,13},{10,... | collective-permute-start | bytes 1179656 | tf_op jit(solution)/shard_map/ppermute | solution.py:233
  214.0 28.7 %collective-permute-start.3 = (f32[2,48,1024]{2,1,0:T(8,128)S(1)}, f32[2,48,1024]{2,1,0:T(8,128)}, u32[]{:S(2)}, u32[]{:S(2)}) collective-permute-start(f32[2,48,1024]{2,1,0:T(8,128)S(1)} %get-tuple-element.39), channel_id=1, source_target_pairs={{0,8},{1,9},{2,10},{3,11},{4,12},{5,13},{6,14},{7,15},{8,0},{9,1},... | collective-permute-start | bytes 1179656 | tf_op jit(solution)/shard_map/ppermute | solution.py:233
  218.0 24.7 %collective-permute-start.4 = (f32[2,48,1024]{2,1,0:T(8,128)S(1)}, f32[2,48,1024]{2,1,0:T(8,128)}, u32[]{:S(2)}, u32[]{:S(2)}) collective-permute-start(f32[2,48,1024]{2,1,0:T(8,128)S(1)} %get-tuple-element.38), channel_id=1, source_target_pairs={{0,12},{1,13},{2,14},{3,15},{4,8},{5,9},{6,10},{7,11},{8,4},{9,5},... | collective-permute-start | bytes 1179656 | tf_op jit(solution)/shard_map/ppermute | solution.py:233
  220.9 23.6 %collective-permute-start.6 = (f32[2,40,1024]{2,1,0:T(8,128)}, f32[2,40,1024]{2,1,0:T(8,128)}, u32[]{:S(2)}, u32[]{:S(2)}) collective-permute-start(f32[2,40,1024]{2,1,0:T(8,128)} %get-tuple-element.43), channel_id=1, source_target_pairs={{0,4},{1,5},{2,6},{3,7},{4,0},{5,1},{6,2},{7,3},{8,12},{9,13},{10,... | collective-permute-start | bytes 983048 | tf_op jit(solution)/shard_map/ppermute | solution.py:233
  221.5 29.1 %collective-permute-start.7 = (f32[2,40,1024]{2,1,0:T(8,128)}, f32[2,40,1024]{2,1,0:T(8,128)}, u32[]{:S(2)}, u32[]{:S(2)}) collective-permute-start(f32[2,40,1024]{2,1,0:T(8,128)} %get-tuple-element.42), channel_id=1, source_target_pairs={{0,8},{1,9},{2,10},{3,11},{4,12},{5,13},{6,14},{7,15},{8,0},{9,1},... | collective-permute-start | bytes 983048 | tf_op jit(solution)/shard_map/ppermute | solution.py:233
  234.0 6.1 %copy-start.3 = (f32[2,40,1024]{2,1,0:T(8,128)S(1)}, f32[2,40,1024]{2,1,0:T(8,128)}, u32[]{:S(2)}) copy-start(f32[2,40,1024]{2,1,0:T(8,128)} %get-tuple-element.41) | copy-start | bytes 983044
  240.1 17.3 %collective-permute-start.8 = (f32[2,40,1024]{2,1,0:T(8,128)S(1)}, f32[2,40,1024]{2,1,0:T(8,128)S(1)}, u32[]{:S(2)}, u32[]{:S(2)}) collective-permute-start(f32[2,40,1024]{2,1,0:T(8,128)S(1)} %copy-done.3), channel_id=1, source_target_pairs={{0,12},{1,13},{2,14},{3,15},{4,8},{5,9},{6,10},{7,11},{8,4},{9,5},... | collective-permute-start | bytes 983048 | tf_op jit(solution)/shard_map/ppermute | solution.py:233
  242.7 16.0 %collective-permute-start.10 = (f32[8,24,1024]{2,1,0:T(8,128)S(1)}, f32[8,24,1024]{2,1,0:T(8,128)S(1)}, u32[]{:S(2)}, u32[]{:S(2)}) collective-permute-start(f32[8,24,1024]{2,1,0:T(8,128)S(1)} %get-tuple-element.35), channel_id=1, source_target_pairs={{0,1},{1,0},{2,3},{3,2},{4,5},{5,4},{6,7},{7,6},{8,9},{9,8},{10,11... | collective-permute-start | bytes 2359304 | tf_op jit(solution)/shard_map/ppermute | solution.py:233
  244.3 22.4 %collective-permute-start.5 = (f32[48,1024]{1,0:T(8,128)S(1)}, f32[48,1024]{1,0:T(8,128)S(1)}, u32[]{:S(2)}, u32[]{:S(2)}) collective-permute-start(f32[48,1024]{1,0:T(8,128)S(1)} %slice_bitcast_fusion), channel_id=1, source_target_pairs={{0,2},{1,3},{2,0},{3,1},{4,6},{5,7},{6,4},{7,5},{8,10},{9,11},{10,... | collective-permute-start | bytes 589832 | tf_op jit(solution)/shard_map/ppermute | solution.py:233
  259.7 19.7 %all-to-all-start.4 = ((f32[8,24,1024]{2,1,0:T(8,128)}), f32[8,24,1024]{2,1,0:T(8,128)S(1)}, u32[]{:S(2)}, u32[]{:S(2)}) async-start(f32[8,24,1024]{2,1,0:T(8,128)} %add.157), calls=%async_computation.4 | async-start | bytes 1572864 | tf_op jit(solution)/shard_map/all_to_all | solution.py:267
  263.3 16.1 %collective-permute-start.9 = (f32[40,1024]{1,0:T(8,128)S(1)}, f32[40,1024]{1,0:T(8,128)S(1)}, u32[]{:S(2)}, u32[]{:S(2)}) collective-permute-start(f32[40,1024]{1,0:T(8,128)S(1)} %slice_bitcast_fusion.2), channel_id=1, source_target_pairs={{0,2},{1,3},{2,0},{3,1},{4,6},{5,7},{6,4},{7,5},{8,10},{9,11},{10,... | collective-permute-start | bytes 491528 | tf_op jit(solution)/shard_map/ppermute | solution.py:233
